TPU v7x, 256 devices: a 2x2x32 block of a 4x8x32 slice. The times are simulated.
256 devices in a mesh: grp: 4 (over y, x), seq: 32 (over z), head: 2 (over core).
Axes of the slice: x: 2, y: 2, z: 32, core: 2. Of those that a mesh axis runs over, the one named last changes fastest.
The devices are a block of a 4x8x32 slice.
Arguments:
- inputs: float32 [32768, 4096], P(('grp', 'seq'), 'head'), parts along dimension 0, may hold values from -6 to 6
- rates: float32 [64, 32768], P('head', ('grp', 'seq')), parts along dimension 1, may hold values from 0.5 to 2
- decay_rate: float32 [64], P('head'), may hold values from 0.00012207031 to 0.03
- skip: float32 [64], P('head'), may hold values from 0.5 to 1.5
- keys_b: float32 [32768, 128], P(('grp', 'seq')), parts along dimension 0, may hold values from -0.5 to 0.5
- keys_c: float32 [32768, 128], P(('grp', 'seq')), parts along dimension 0, may hold values from -0.5 to 0.5
- grad_out: float32 [32768, 4096], P(('grp', 'seq'), 'head'), parts along dimension 0, may hold values from -6 to 6
Outputs:
- output: float32 [32768, 4096], P(('grp', 'seq'), 'head'), parts along dimension 0
- grad_inputs: float32 [32768, 4096], P(('grp', 'seq'), 'head'), parts along dimension 0
- input_key_gradient: float32 [32768, 128], P(('grp', 'seq')), parts along dimension 0
- output_key_gradient: float32 [32768, 128], P(('grp', 'seq')), parts along dimension 0
There are 4 independent parts, one for each index of `grp`. A program takes and returns all parts, laid end to end along the dimension named above; an argument that names none is the same for every part. Nothing has to cross between parts.
All inputs are finite; a program needn't handle non-finite values.
Results may differ from a plain program's by a relative error of at most 0.00016.
Values sent between devices are 32-bit elements; how exact they have to be, the bound alone decides.
No kernel may reach another device: no remote copies, remote signals or barrier semaphores. Data moves between devices by JAX's collectives and lax.ppermute only.
A program may use at most 192 MiB of HBM per device.

v0:
```python
import jax
import jax.numpy as jnp
from jax import lax
from jax.sharding import PartitionSpec as P

Q = 128


HIGH = lax.Precision.HIGHEST


def carried_in(array, axis, combine, identity, reverse):
    size, mine = (lax.axis_size(axis), lax.axis_index(axis))
    everything = jax.tree.map(lambda part: lax.all_gather(part, axis), array)
    start = jax.tree.map(
        lambda part, zero: jnp.broadcast_to(jnp.asarray(zero, part.dtype), part.shape),
        array,
        identity,
    )

    def turn(k, before):
        at = size - 1 - k if reverse else k
        reached = at > mine if reverse else at < mine
        new = combine(before, jax.tree.map(lambda part: part[at], everything))
        return jax.tree.map(lambda a, b: jnp.where(reached, a, b), new, before)

    return lax.fori_loop(0, size, turn, start)


def from_everyone(array, axis):
    copies = jnp.broadcast_to(array, (lax.axis_size(axis), *array.shape))
    return lax.all_to_all(copies, axis, split_axis=0, concat_axis=0, tiled=True)


def of_everyone(array, axis):
    return from_everyone(array, axis).sum(axis=0)


def mixed_output(form, left, right):
    return jnp.einsum(form, left, right, precision=HIGH)


def decays(rates, decay_rate, block):
    heads, length = rates.shape
    count = length // block
    logs = -(decay_rate[:, None] * rates).reshape(heads, count, block)
    inner = jnp.cumsum(logs, axis=2)
    ends = inner[:, :, -1]
    starts = jnp.cumsum(ends, axis=1) - ends
    total = jnp.sum(ends, axis=1)
    rows = lax.broadcasted_iota(jnp.int32, (block, block), 0)
    cols = lax.broadcasted_iota(jnp.int32, (block, block), 1)
    gap = inner[:, :, :, None] - inner[:, :, None, :]
    within = jnp.where(rows >= cols, jnp.exp(jnp.where(rows >= cols, gap, 0.0)), 0.0)
    upper = lax.broadcasted_iota(jnp.int32, (count, count), 0)
    lower = lax.broadcasted_iota(jnp.int32, (count, count), 1)
    span = starts[:, :, None] - starts[:, None, :] - ends[:, None, :]
    across = jnp.where(upper > lower, jnp.exp(jnp.where(upper > lower, span, 0.0)), 0.0)
    return (inner, ends, starts, total, within, across)


def layer(inputs, rates, decay_rate, skip, keys_b, keys_c, grads, incoming, outgoing, block):
    length, heads, width = inputs.shape
    count = length // block
    state_size = keys_b.shape[1]
    inner, ends, starts, total, within, across = decays(rates, decay_rate, block)
    input_rows = inputs.reshape(count, block, heads, width)
    dys = grads.reshape(count, block, heads, width)
    input_key_rows = keys_b.reshape(count, block, state_size)
    output_key_rows = keys_c.reshape(count, block, state_size)
    steps = rates.reshape(heads, count, block)
    scores = mixed_output("ctn,csn->cts", output_key_rows, input_key_rows)
    weighted = within * scores[None]
    intra = mixed_output("hcts,cshp->cthp", weighted * steps[:, :, None, :], input_rows)
    tail_segment = jnp.transpose(jnp.exp(ends[:, :, None] - inner) * steps, (1, 2, 0))[..., None]
    growth = jnp.transpose(jnp.exp(inner), (1, 2, 0))[..., None]
    stretch_states = mixed_output("cshp,csn->hcpn", input_rows * tail_segment, input_key_rows)
    entering_state = mixed_output("hck,hkpn->hcpn", across, stretch_states)
    closing = jnp.exp(total[:, None] - starts - ends)
    final = mixed_output("hc,hcpn->hpn", closing, stretch_states)
    seg_decay = jnp.exp(total)
    first_state = incoming(seg_decay, final)
    entering_state = entering_state + jnp.exp(starts)[:, :, None, None] * first_state[:, None]
    output = (
        intra
        + mixed_output("hcpn,ctn->cthp", entering_state, output_key_rows) * growth
        + skip[None, None, :, None] * input_rows
    )
    scaled_output_gradient = dys * growth
    pushed = mixed_output("cshp,csn->hcpn", scaled_output_gradient, output_key_rows)
    later = mixed_output("hkc,hkpn->hcpn", across, pushed)
    opening = mixed_output("hc,hcpn->hpn", jnp.exp(starts), pushed)
    last_adjoint = outgoing(seg_decay, opening)
    adjoint_state = later + closing[:, :, None, None] * last_adjoint[:, None]
    step_t = jnp.transpose(steps, (1, 2, 0))[..., None]
    grad_x = mixed_output("hcst,cshp->cthp", weighted, dys) * step_t
    grad_x = (
        grad_x
        + mixed_output("hcpn,ctn->cthp", adjoint_state, input_key_rows) * tail_segment
        + skip[None, None, :, None] * dys
    )
    products = jnp.einsum("cahp,cbhp->hcab", dys, input_rows, precision=HIGH)
    masked_scores = within * products * steps[:, :, None, :]
    output_key_gradient = mixed_output(
        "qsgm,smd->sgd", masked_scores, input_key_rows
    ) + mixed_output("jizk,zjky->jiy", scaled_output_gradient, entering_state)
    input_key_gradient = mixed_output(
        "megv,egs->evs", masked_scores, output_key_rows
    ) + mixed_output("jizk,zjky->jiy", input_rows * tail_segment, adjoint_state)
    return (
        output.reshape(length, heads, width),
        grad_x.reshape(length, heads, width),
        input_key_gradient.reshape(length, state_size),
        output_key_gradient.reshape(length, state_size),
    )


def join_forward(earlier, later):
    return (earlier[0] * later[0], later[0][:, None, None] * earlier[1] + later[1])


def join_backward(earlier, later):
    return (earlier[0] * later[0], later[1] + later[0][:, None, None] * earlier[1])


def body(inputs, rates, decay_rate, skip, keys_b, keys_c, grad_out):
    tokens = inputs.shape[0]
    heads = rates.shape[0]
    width = inputs.shape[1] // heads
    block = Q
    values = inputs.reshape(tokens, heads, width)
    grads = grad_out.reshape(tokens, heads, width)

    def carry_in(seg_decay, states):
        result = carried_in(
            (seg_decay, states),
            "seq",
            join_forward,
            (jnp.ones_like(seg_decay), jnp.zeros_like(states)),
            False,
        )
        return result[1]

    def carry_back(seg_decay, states):
        result = carried_in(
            (seg_decay, states),
            "seq",
            join_backward,
            (jnp.ones_like(seg_decay), jnp.zeros_like(states)),
            True,
        )
        return result[1]

    output, grad_x, term_b, term_c = layer(
        values, rates, decay_rate, skip, keys_b, keys_c, grads, carry_in, carry_back, block
    )
    input_key_gradient, output_key_gradient = (
        of_everyone(term_b, "head"),
        of_everyone(term_c, "head"),
    )
    return (
        output.reshape(tokens, heads * width),
        grad_x.reshape(tokens, heads * width),
        input_key_gradient,
        output_key_gradient,
    )


def solution(mesh):
    in_specs = (
        P(("grp", "seq"), "head"),
        P("head", ("grp", "seq")),
        P("head"),
        P("head"),
        P(("grp", "seq"), None),
        P(("grp", "seq"), None),
        P(("grp", "seq"), "head"),
    )
    out_specs = (
        P(("grp", "seq"), "head"),
        P(("grp", "seq"), "head"),
        P(("grp", "seq"), None),
        P(("grp", "seq"), None),
    )
    return jax.shard_map(body, mesh=mesh, in_specs=in_specs, out_specs=out_specs, check_vma=False)
```

profile of v0, /device:TPU:37, one launch (start us, length us, event | category | flops | bytes accessed | tf_op | source)
XLA Modules:
  0.0 943.6 jit_solution(8993118020488764192)
XLA Ops:
  18.4 8.9 fusion.50
  30.6 3.3 reshape_reshape.14
  33.9 3.5 fusion.44
  38.8 8.9 fusion.47
  53.3 72.5 %all-reduce = f32[1024]{0:T(1024)S(1)} all-reduce(f32[1024]{0:T(1024)S(1)} %exponential_dynamic-update-slice_fusion), channel_id=2, replica_groups=mesh['grp'=4,'seq'=32,'head'=2] {'seq'}, use_global_device_ids=true, to_apply=%add | all-reduce | flops 1024 | bytes 8192
  131.4 4.9 fusion.6
  136.3 8.7 multiply_reduce_fusion
  145.0 272.9 %all-gather.6.cloned.1.call-done = f32[1024,64,128]{2,1,0:T(8,128)} async-done(((f32[32,64,128]{2,1,0:T(8,128)}), f32[1024,64,128]{2,1,0:T(8,128)}) %all-gather.6.cloned.1.call-update) | async-done | bytes 33554448 | tf_op jit(solution)/shard_map/all_gather | solution.py:14
  418.0 108.5 %while.30 = (s32[]{:T(128)}, f32[32,64,128]{2,1,0:T(8,128)}, s32[]{:T(128)}, f32[32,32]{1,0:T(8,128)}, f32[32,32,64,128]{3,2,1,0:T(8,128)}, /*index=5*/s32[]{:T(128)}, s32[]{:T(128)}) while((s32[]{:T(128)}, f32[32,64,128]{2,1,0:T(8,128)}, s32[]{:T(128)}, f32[32,32]{1,0:T(8,128)}, f32[32,32,64,128]{3,2,1,0:T(8,128)}, ...), condition=%wide.region_4.5_spmd.clone, body=%wide.region_3.4_spmd.clone.sunk | while | flops 1048580 | bytes 3146225 | solution.py:27
  526.5 13.6 %multiply_add_fusion.1 = f32[32,2,64,128]{3,1,2,0:T(2,128)S(1)} fusion(f32[32,2,64,128]{3,2,0,1:T(8,128)} %copy-done.5, f32[32,64,128]{2,1,0:T(8,128)} %get-tuple-element.230, f32[32,2]{1,0:T(8,128)S(1)} %copy-done.14, pred[2,2]{0,1:T(4,128)(4,1)S(1)} %copy-done.17, f32[32,2]{1,0:T(8,128)S(1)} %copy-done.12, f32[32,2]{1,0:T(8,128)S(1)} %copy-done.11, ...), kind=kOutput, calls=%fused_computation.23 | convolution fusion | flops 13632000 | bytes 5243908 | tf_op jit(solution)/shard_map/hck,hkpn->hcpn/dot_general | solution.py:40
  540.2 4.2 fusion.53
  547.5 247.1 %all-gather.8.cloned.1.call-done = f32[1024,64,128]{2,1,0:T(8,128)} async-done(((f32[32,64,128]{2,1,0:T(8,128)}), f32[1024,64,128]{2,1,0:T(8,128)}) %all-gather.8.cloned.1.call-update) | async-done | bytes 33554448 | tf_op jit(solution)/shard_map/all_gather | solution.py:14
  794.7 69.6 %while.31 = (s32[]{:T(128)}, f32[32,64,128]{2,1,0:T(8,128)S(1)}, s32[]{:T(128)}, f32[32,32,64,128]{3,2,1,0:T(8,128)}, f32[32,32]{1,0:T(8,128)}, /*index=5*/s32[]{:T(128)}, s32[]{:T(128)}, s32[]{:T(128)}, s32[]{:T(128)}) while((s32[]{:T(128)}, f32[32,64,128]{2,1,0:T(8,128)S(1)}, s32[]{:T(128)}, f32[32,32,64,128]{3,2,1,0:T(8,128)}, ...), condition=%wide.region_6.7_spmd.clone, body=%wide.region_5.6_spmd.clone.sunk | while | flops 1048584 | bytes 3146287 | solution.py:27
  864.3 12.0 %multiply_add_fusion = f32[32,2,64,128]{3,1,2,0:T(2,128)S(1)} fusion(f32[32,2,64,128]{3,2,0,1:T(8,128)} %copy-done.4, f32[32,64,128]{2,1,0:T(8,128)S(1)} %get-tuple-element.231, f32[32,2]{1,0:T(8,128)S(1)} %copy-done.13, pred[2,2]{0,1:T(4,128)(4,1)S(1)} %copy-done.17, f32[32,2]{1,0:T(8,128)S(1)} %copy-done.12, f32[32,2]{1,0:T(8,128)S(1)} %copy-done.11, ...), kind=kOutput, calls=%fused_computation.22 | convolution fusion | flops 13632000 | bytes 5243908 | tf_op jit(solution)/shard_map/hkc,hkpn->hcpn/dot_general | solution.py:40
  876.3 3.5 fusion.58
  879.9 3.2 fusion.15
  884.1 4.3 all-to-all-start.1
  888.8 9.2 fusion.8
  898.0 5.8 copy.153
  903.7 5.0 reshape.109
  908.7 11.1 %fusion.10 = f32[2,128,32,64]{1,3,2,0:T(8,128)} fusion(f32[2,32,64,128]{3,2,1,0:T(8,128)} %fusion.19, f32[2,128,32,64]{1,0,3,2:T(2,128)S(1)} %reshape_reshape.12, f32[32,2,128,128]{3,2,1,0:T(8,128)} %get-tuple-element.305, f32[32]{0:T(128)S(1)} %copy-done.15, f32[2,128,32]{1,2,0:T(8,128)S(1)} %get-tuple-element.306), kind=kOutput, calls=%fused_computation.19 | convolution fusion | flops 807403520 | bytes 10518656 | tf_op jit(solution)/shard_map/hcts,cshp->cthp/dot_general | solution.py:40
  919.8 5.5 copy.152
  925.3 5.0 reshape.108
  931.0 3.5 all-to-all-start
  (209 shorter events, 210.4 us)
Async XLA Ops:
  7.2 7.9 copy-start
  7.2 410.8 %all-gather.6.cloned.1.call-start = ((), (), s32[]{:S(2)}) async-start(), calls=%async_computation.2 | async-start | bytes 34603008 | tf_op jit(solution)/shard_map/all_gather | solution.py:14
  17.0 1.3 copy-start.5
  27.3 767.3 %all-gather.8.cloned.1.call-start = ((), (), s32[]{:S(2)}) async-start(), calls=%async_computation.3 | async-start | bytes 34603008 | tf_op jit(solution)/shard_map/all_gather | solution.py:14
  30.6 3.3 copy-start.3
  37.4 1.4 copy-start.4
  38.8 9.0 copy-start.9
  38.8 13.1 %copy-start.16 = (u32[256]{0:T(256)S(1)}, u32[256]{0:T(256)}, u32[]{:S(2)}) copy-start(u32[256]{0:T(256)} %constant.83) | copy-start | bytes 3076
  131.4 4.9 copy-start.1
  131.4 4.9 copy-start.8
  418.0 108.5 %copy-start.11 = (f32[32,2]{1,0:T(8,128)S(1)}, f32[32,2]{1,0:T(8,128)}, u32[]{:S(2)}) copy-start(f32[32,2]{1,0:T(8,128)} %copy.111) | copy-start | bytes 772
  418.0 108.5 %copy-start.12 = (f32[32,2]{1,0:T(8,128)S(1)}, f32[32,2]{1,0:T(8,128)}, u32[]{:S(2)}) copy-start(f32[32,2]{1,0:T(8,128)} %copy.112) | copy-start | bytes 772
  418.0 108.5 %copy-start.14 = (f32[32,2]{1,0:T(8,128)S(1)}, f32[32,2]{1,0:T(8,128)}, u32[]{:S(2)}) copy-start(f32[32,2]{1,0:T(8,128)} %copy.117) | copy-start | bytes 772
  418.0 108.5 %copy-start.17 = (pred[2,2]{0,1:T(4,128)(4,1)S(1)}, pred[2,2]{0,1:T(4,128)(4,1)}, u32[]{:S(2)}) copy-start(pred[2,2]{0,1:T(4,128)(4,1)} %iota_compare_fusion.1) | copy-start | bytes 16
  526.5 13.6 %copy-start.2 = (f32[2,128,32,64]{1,0,3,2:T(2,128)S(1)}, f32[2,128,32,64]{1,0,3,2:T(2,128)}, u32[]{:S(2)}) copy-start(f32[2,128,32,64]{1,0,3,2:T(2,128)} %reshape_reshape.14) | copy-start | bytes 6291460
  794.7 69.6 %copy-start.13 = (f32[32,2]{1,0:T(8,128)S(1)}, f32[32,2]{1,0:T(8,128)}, u32[]{:S(2)}) copy-start(f32[32,2]{1,0:T(8,128)} %copy.127) | copy-start | bytes 772
  879.8 3.2 copy-start.6
  879.8 3.2 copy-start.7
  879.8 8.9 copy-start.10
  879.9 8.9 copy-start.15
  884.1 46.2 %all-to-all-start.1 = ((f32[2,256,128]{2,1,0:T(8,128)}), f32[2,256,128]{2,1,0:T(8,128)S(1)}, u32[]{:S(2)}, u32[]{:S(2)}) async-start(f32[2,256,128]{2,1,0:T(8,128)} %broadcast_in_dim.51), calls=%async_computation.1 | async-start | bytes 524288 | tf_op jit(solution)/shard_map/all_to_all | solution.py:32
  931.0 4.7 all-to-all-start
Sparse Core Ops, SparseCore 0:
  27.4 390.4 all-gather.5
  419.8 374.8 all-gather.7
where the time goes:
time: 954 us; the launch traced here: 944 us
  waiting for transfers between devices  521 us (55%)
  other arithmetic  144 us (15%)
  matrix products  93.1 us (10%)
  local copies, waits for them, and re-layouts  88.6 us (9%)
  blocking collectives  72.5 us (8%)
  between operations  15.5 us (2%)
    all_gather x2, waiting for transfers between devices, carried_in(): everything = jax.tree.map(lambda part: lax.all_gather(part, axis), array)  520 us
    select_n x64, other arithmetic, turn(): return jax.tree.map(lambda a, b: jnp.where(reached, a, b), new, before)  133 us
    dot_general x15, matrix products, mixed_output(): return jnp.einsum(form, left, right, precision=HIGH)  84.4 us
    unnamed x1, blocking collectives  72.5 us
    unnamed x45, local copies, waits for them, and re-layouts  30.4 us
    mul x32, local copies, waits for them, and re-layouts, join_backward(): later[0][:, None, None] * earlier[1]  22 us
    mul x32, local copies, waits for them, and re-layouts, join_forward(): later[0][:, None, None] * earlier[1] + later[1]  21.8 us
  transfers between devices with their start and end apart: 4, of which 3 were waited for; matrix products, arithmetic and copies ran while one was open for 23% of the time, Pallas kernels for 0%

commit v1 on v0

v1 whole, which is shorter than its diff:
```python
import functools

import jax
import jax.numpy as jnp
from jax import lax
from jax.experimental import pallas as pl
from jax.experimental.pallas import tpu as pltpu
from jax.sharding import PartitionSpec as P

HIGHEST = lax.Precision.HIGHEST
LANES = 256
LEVELS = 3


def halves(a):
    high = a.astype(jnp.bfloat16)
    return high, (a - high.astype(jnp.float32)).astype(jnp.bfloat16)


def dot3(a, b, dims=(((1,), (0,)), ((), ()))):
    dot = functools.partial(lax.dot_general, dimension_numbers=dims, preferred_element_type=jnp.float32)
    return dot(a[0], b[0]) + (dot(a[0], b[1]) + dot(a[1], b[0]))


NT = (((1,), (1,)), ((), ()))
TN = (((0,), (0,)), ((), ()))


def spread(columns, first, width, lanes):
    heads = columns.shape[1]
    row = lax.broadcasted_iota(jnp.int32, (heads, lanes), 0)
    lane = lax.broadcasted_iota(jnp.int32, (heads, lanes), 1)
    chosen = jnp.where(row == first + lane // width, 1.0, 0.0).astype(jnp.float32)
    return jnp.dot(columns, chosen, precision=HIGHEST, preferred_element_type=jnp.float32)


def states_kernel(width, x_ref, dy_ref, tail_ref, growth_ref, b_ref, c_ref, out_ref):
    first = pl.program_id(0) * (LANES // width)
    xs = x_ref[...] * spread(tail_ref[...], first, width, LANES)
    ys = dy_ref[...] * spread(growth_ref[...], first, width, LANES)
    out_ref[0] = dot3(halves(b_ref[...]), halves(xs), TN)
    out_ref[1] = dot3(halves(c_ref[...]), halves(ys), TN)


def local_kernel(width, x_ref, dy_ref, inner_t_ref, rates_t_ref, inner_ref, rates_ref, skip_ref, b_ref, c_ref, y_ref, gx_ref, keys_ref, cb_ref, bc_ref, sum_ref):
    step = pl.program_id(0)
    tokens = x_ref.shape[0]
    per = LANES // width

    @pl.when(step == 0)
    def _():
        b, c = halves(b_ref[...]), halves(c_ref[...])
        cb_ref[...] = dot3(c, b, NT)
        bc_ref[...] = dot3(b, c, NT)
        sum_ref[...] = jnp.zeros_like(sum_ref)

    row = lax.broadcasted_iota(jnp.int32, (tokens, tokens), 0)
    col = lax.broadcasted_iota(jnp.int32, (tokens, tokens), 1)
    lane = lax.broadcasted_iota(jnp.int32, (tokens, 2 * width), 1)
    total = sum_ref[...]
    for pair in range(per // 2):
        at = slice(pair * 2 * width, (pair + 1) * 2 * width)
        x, dy = x_ref[:, at], dy_ref[:, at]
        y = skip_ref[:, at] * x
        gx = skip_ref[:, at] * dy
        x_parts, dy_parts = halves(x), halves(dy)
        for side in range(2):
            i = pair * 2 + side
            mine = (lane < width) if side == 0 else (lane >= width)
            zero = jnp.zeros((), jnp.bfloat16)
            x_own = tuple(jnp.where(mine, part, zero) for part in x_parts)
            dy_own = tuple(jnp.where(mine, part, zero) for part in dy_parts)
            down = spread(inner_t_ref[...], step * per + i, tokens, tokens)
            dt_down = spread(rates_t_ref[...], step * per + i, tokens, tokens)
            across = inner_ref[0, i : i + 1, :]
            gap = down - across
            within = jnp.where(row >= col, jnp.exp(jnp.minimum(gap, 0.0)), 0.0) * rates_ref[0, i : i + 1, :]
            turned = jnp.where(col >= row, jnp.exp(jnp.minimum(-gap, 0.0)), 0.0) * dt_down
            y = y + dot3(halves(within * cb_ref[...]), x_own)
            gx = gx + dot3(halves(turned * bc_ref[...]), dy_own)
            total = total + within * dot3(dy_own, x_parts, NT)
        y_ref[:, at] = y
        gx_ref[:, at] = gx
    sum_ref[...] = total

    @pl.when(step == pl.num_programs(0) - 1)
    def _():
        parts = halves(sum_ref[...])
        keys_ref[:tokens] = dot3(parts, halves(c_ref[...]), TN)
        keys_ref[tokens:] = dot3(parts, halves(b_ref[...]))


def finish_kernel(width, x_ref, dy_ref, tail_ref, growth_ref, b_ref, c_ref, low_ref, high_ref, y_ref, gx_ref, terms_ref, out_ref, grad_ref, keys_ref):
    step = pl.program_id(0)
    tokens = x_ref.shape[0]
    first = step * (LANES // width)
    tail = spread(tail_ref[...], first, width, LANES)
    growth = spread(growth_ref[...], first, width, LANES)
    entering, adjoint = (halves(jnp.concatenate([low_ref[i], high_ref[i]], axis=0)) for i in range(2))
    out_ref[...] = y_ref[...] + growth * dot3(halves(c_ref[...]), entering)
    grad_ref[...] = gx_ref[...] + tail * dot3(halves(b_ref[...]), adjoint)

    @pl.when(step == 0)
    def _():
        keys_ref[...] = terms_ref[...]

    keys_ref[:tokens] += dot3(halves(x_ref[...] * tail), adjoint, NT)
    keys_ref[tokens:] += dot3(halves(dy_ref[...] * growth), entering, NT)


def whole(shape):
    return pl.BlockSpec(shape, lambda i: (0,) * len(shape))


def span(weights, table):
    return jnp.exp(jnp.dot(weights, table, precision=HIGHEST))


def exchange(states, log_decay, spread_lanes, axis, meanwhile):
    size, mine = lax.axis_size(axis), lax.axis_index(axis)
    heads = log_decay.shape[0]
    table = jnp.zeros((size, 128), jnp.float32)
    table = lax.dynamic_update_slice(table, jnp.pad(log_decay, (0, 128 - heads))[None], (mine, 0))
    seg = jnp.arange(size)
    steps = size.bit_length() - 1
    tables = []
    for k in range(steps):
        table = table + lax.ppermute(table, axis, [(i, i ^ (1 << k)) for i in range(size)])
        tables.append(table)

    def weights(masks, known):
        rows = span(jnp.stack(masks).astype(jnp.float32), known)
        return jnp.dot(rows, spread_lanes, precision=HIGHEST)

    kept, sides = [], []
    now = states
    for k in range(LEVELS):
        pairs = [(i, i ^ (1 << k)) for i in range(size)]
        right = ((mine >> k) & 1) == 1
        base = (mine >> (k + 1)) << (k + 1)
        half = 1 << k
        both = weights(
            [(seg >= base) & (seg < base + half), (seg >= base + half) & (seg < base + 2 * half)], tables[k]
        )
        over_left, over_right = both[0:1], both[1:2]
        rows = now.shape[1] // 2
        low, high = now[:, :rows], now[:, rows:]
        own = jnp.where(right, high, low)
        got = lax.ppermute(jnp.where(right, low, high), axis, pairs)
        left_part, right_part = jnp.where(right, got, own), jnp.where(right, own, got)
        now = jnp.stack(
            [over_right * left_part[0] + right_part[0], left_part[1] + over_left * right_part[1]]
        )
        kept.append((left_part[0], right_part[1], over_left, over_right))
        sides.append((pairs, right))

    block = 1 << LEVELS
    count = size // block
    place = mine // block
    forward = jnp.zeros_like(now[0])
    backward = jnp.zeros_like(now[0])
    masks, received = [], []
    for d in range(1, count):
        pairs = [(i, (i + block * d) % size) for i in range(size)]
        received.append(lax.ppermute(jnp.where(place + d < count, now[0], now[1]), axis, pairs))
        source = (place - d) % count
        first, last = jnp.minimum(source, place), jnp.maximum(source, place)
        masks.append((seg // block > first) & (seg // block < last))
    between = weights(masks, tables[-1])
    aside = meanwhile(now)
    received, aside = lax.optimization_barrier((received, aside))
    for d in range(1, count):
        term = between[d - 1 : d] * received[d - 1]
        forward = forward + jnp.where(place >= d, term, 0.0)
        backward = backward + jnp.where(place >= d, 0.0, term)

    for k in reversed(range(LEVELS)):
        left_sum, right_sum, over_left, over_right = kept[k]
        pairs, right = sides[k]
        to_left = jnp.stack([forward, over_right * backward + right_sum])
        to_right = jnp.stack([over_left * forward + left_sum, backward])
        own = jnp.where(right, to_right, to_left)
        got = lax.ppermute(jnp.where(right, to_left, to_right), axis, pairs)
        low, high = jnp.where(right, got, own), jnp.where(right, own, got)
        if k:
            forward, backward = (jnp.concatenate([low[i], high[i]], axis=0) for i in range(2))
    return (low, high), aside


def body(inputs, rates, decay_rate, skip, keys_b, keys_c, grad_out):
    tokens, lanes = inputs.shape
    heads = rates.shape[0]
    width = lanes // heads
    state_size = keys_b.shape[1]
    grid = lanes // LANES
    per = LANES // width

    logs = -(decay_rate[:, None] * rates)
    upto = jnp.triu(jnp.ones((tokens, tokens), jnp.float32))
    inner = jnp.dot(logs, upto, precision=HIGHEST)
    total = jnp.sum(logs, axis=1)
    inner_t = inner.T
    rates_t = rates.T
    growth_t = jnp.exp(inner_t)
    tail_t = jnp.exp(jnp.minimum(total[None, :] - inner_t, 0.0)) * rates_t
    head_of = jnp.arange(lanes) // width
    spread_lanes = (jnp.arange(128)[:, None] == head_of[None, :]).astype(jnp.float32)
    skip_lanes = jnp.dot(jnp.pad(skip, (0, 128 - heads))[None], spread_lanes, precision=HIGHEST)

    tile = pl.BlockSpec((tokens, LANES), lambda i: (0, i))
    state_tile = pl.BlockSpec((2, state_size, LANES), lambda i: (0, 0, i))
    half_tile = pl.BlockSpec((2, state_size // 2, LANES), lambda i: (0, 0, i))
    columns = whole((tokens, heads))
    keys = whole((tokens, state_size))
    big = jax.ShapeDtypeStruct((tokens, lanes), jnp.float32)
    params = pltpu.CompilerParams(dimension_semantics=("arbitrary",))

    states = pl.pallas_call(
        functools.partial(states_kernel, width),
        grid=(grid,),
        in_specs=[tile, tile, columns, columns, keys, keys],
        out_specs=state_tile,
        out_shape=jax.ShapeDtypeStruct((2, state_size, lanes), jnp.float32),
        compiler_params=params,
        cost_estimate=pl.CostEstimate(flops=12 * tokens * state_size * lanes, bytes_accessed=6 << 20, transcendentals=0),
        name="states",
    )(inputs, grad_out, tail_t, growth_t, keys_b, keys_c)

    small = pl.BlockSpec((1, per, tokens), lambda i: (i, 0, 0))
    local = pl.pallas_call(
        functools.partial(local_kernel, width),
        grid=(grid,),
        in_specs=[tile, tile, columns, columns, small, small, pl.BlockSpec((1, LANES), lambda i: (0, i)), keys, keys],
        out_specs=[tile, tile, whole((2 * tokens, state_size))],
        out_shape=[big, big, jax.ShapeDtypeStruct((2 * tokens, state_size), jnp.float32)],
        scratch_shapes=[pltpu.VMEM((tokens, tokens), jnp.float32)] * 3,
        compiler_params=params,
        cost_estimate=pl.CostEstimate(flops=18 * tokens * tokens * lanes, bytes_accessed=8 << 20, transcendentals=2 * tokens * tokens * heads),
        name="local",
    )
    by_step = inner.reshape(grid, per, tokens), rates.reshape(grid, per, tokens)

    def meanwhile(after):
        x, _ = lax.optimization_barrier((inputs, after))
        return local(x, grad_out, inner_t, rates_t, *by_step, skip_lanes, keys_b, keys_c)

    (low, high), (y, gx, terms) = exchange(states, total, spread_lanes, "seq", meanwhile)

    output, grad_x, key_terms = pl.pallas_call(
        functools.partial(finish_kernel, width),
        grid=(grid,),
        in_specs=[tile, tile, columns, columns, keys, keys, half_tile, half_tile, tile, tile, whole((2 * tokens, state_size))],
        out_specs=[tile, tile, whole((2 * tokens, state_size))],
        out_shape=[big, big, jax.ShapeDtypeStruct((2 * tokens, state_size), jnp.float32)],
        compiler_params=pltpu.CompilerParams(dimension_semantics=("arbitrary",), vmem_limit_bytes=20 << 20),
        cost_estimate=pl.CostEstimate(flops=24 * tokens * state_size * lanes, bytes_accessed=14 << 20, transcendentals=0),
        name="finish",
    )(inputs, grad_out, tail_t, growth_t, keys_b, keys_c, low, high, y, gx, terms)
    cores = lax.axis_size("head")
    summed = key_terms
    for d in range(1, cores):
        summed = summed + lax.ppermute(key_terms, "head", [(i, (i + d) % cores) for i in range(cores)])
    return output, grad_x, summed[:tokens], summed[tokens:]


def solution(mesh):
    in_specs = (
        P(("grp", "seq"), "head"),
        P("head", ("grp", "seq")),
        P("head"),
        P("head"),
        P(("grp", "seq"), None),
        P(("grp", "seq"), None),
        P(("grp", "seq"), "head"),
    )
    out_specs = (
        P(("grp", "seq"), "head"),
        P(("grp", "seq"), "head"),
        P(("grp", "seq"), None),
        P(("grp", "seq"), None),
    )
    return jax.shard_map(body, mesh=mesh, in_specs=in_specs, out_specs=out_specs, check_vma=False)
```

time: 954 us -> 285 us (0.30)
  waiting for transfers between devices: 521 us -> 125 us
  other arithmetic: 144 us -> 6.7 us
  matrix products: 93.1 us -> 4.42 us
  local copies, waits for them, and re-layouts: 88.6 us -> 3.41 us
  starting transfers between devices: 8.11 us -> 92.3 us
  blocking collectives: 72.5 us -> 0 us
  Pallas kernels: 0 us -> 51.1 us
  between operations: 15.5 us -> 1.28 us
    all_gather x2 -> x0, waiting for transfers between devices: 520 us -> none  [carried_in(): everything = jax.tree.map(lambda part: lax.all_gather(part, axis), array)]
    select_n x64 -> x15, other arithmetic: 133 us -> 4.13 us  [the longest x3 1.75 us: exchange(): got = lax.ppermute(jnp.where(right, low, high), axis, pairs)]
    ppermute x0 -> x15, waiting for transfers between devices: none -> 125 us  [the longest x3 62.2 us: exchange(): got = lax.ppermute(jnp.where(right, to_left, to_right), axis, pairs)]
    ppermute x0 -> x15, starting transfers between devices: none -> 92.3 us  [the longest x5 46.8 us: exchange(): lax.ppermute(table, axis, [(i, i ^ 1 << k) for i in range(size)])]
    dot_general x16 -> x10, matrix products: 93.1 us -> 4.42 us  [the longest x4 1.76 us: weights(): return jnp.dot(rows, spread_lanes, precision=HIGHEST)]
    unnamed x1 -> x0, blocking collectives: 72.5 us -> none
    pallas_call x0 -> x3, Pallas kernels: none -> 51.1 us  [the longest x1 30.9 us: meanwhile(): local(x, grad_out, inner_t, rates_t, *by_step, skip_lanes, keys_b, keys_c)]
    mul x65 -> x0, local copies, waits for them, and re-layouts: 44.4 us -> none  [the longest x32 22 us: join_backward(): later[0][:, None, None] * earlier[1]]
  transfers between devices with their start and end apart: 4 -> 15, of which waited for: 3 -> 10; matrix products, arithmetic and copies ran while one was open for 23% -> 4% of each run, Pallas kernels for 0% -> 14%
where the time goes in v1:
time: 285 us; the launch traced here: 284 us
  waiting for transfers between devices  125 us (44%)
  starting transfers between devices  92.3 us (32%)
  Pallas kernels  51.1 us (18%)
  other arithmetic  6.7 us (2%)
  matrix products  4.42 us (2%)
  local copies, waits for them, and re-layouts  3.41 us (1%)
    ppermute x3, waiting for transfers between devices, exchange(): got = lax.ppermute(jnp.where(right, to_left, to_right), axis, pairs)  62.2 us
    ppermute x5, starting transfers between devices, exchange(): lax.ppermute(table, axis, [(i, i ^ 1 << k) for i in range(size)])  46.8 us
    ppermute x3, starting transfers between devices, exchange(): lax.ppermute(jnp.where(place + d < count, now[0], now[1]), axis, pairs)  33.4 us
    ppermute x3, waiting for transfers between devices, exchange(): lax.ppermute(jnp.where(place + d < count, now[0], now[1]), axis, pairs)  31.8 us
    pallas_call x1, Pallas kernels, meanwhile(): local(x, grad_out, inner_t, rates_t, *by_step, skip_lanes, keys_b, keys_c)  30.9 us
    ppermute x3, waiting for transfers between devices, exchange(): got = lax.ppermute(jnp.where(right, low, high), axis, pairs)  28.7 us
    pallas_call x1, Pallas kernels, body(): pl.pallas_call(functools.partial(finish_kernel, width), grid=(grid,), in_...  10.7 us
    ppermute x3, starting transfers between devices, exchange(): got = lax.ppermute(jnp.where(right, low, high), axis, pairs)  10.3 us
  transfers between devices with their start and end apart: 15, of which 10 were waited for; matrix products, arithmetic and copies ran while one was open for 4% of the time, Pallas kernels for 14%

profile of v1, /device:TPU:37, one launch (start us, length us, event | category | flops | bytes accessed | tf_op | source)
XLA Modules:
  0.0 284.1 jit_solution(17837381112701967198)
XLA Ops:
  1.6 2.8 collective-permute-start
  5.3 1.1 fusion.20
  7.3 9.5 %states.1 = f32[2,128,2048]{2,1,0:T(8,128)} custom-call(f32[256,2048]{1,0:T(8,128)} %x_ref.4, f32[256,2048]{1,0:T(8,128)} %dy_ref.5, f32[256,32]{1,0:T(8,128)} %get-tuple-element.74.tail_ref, f32[256,32]{1,0:T(8,128)} %get-tuple-element.73.growth_ref, f32[256,128]{1,0:T(8,128)} %b_ref.5, f32[256,128]{1,0:T(8,128)} %c_ref.5), custom_call_target="tpu_custom_call" | custom-call | flops 805306368 | bytes 6291456 | tf_op jit(solution)/shard_map/states/pallas_call | solution.py:218
  16.8 1.7 slice_select_fusion.1
  21.1 30.9 %local.1 = (f32[256,2048]{1,0:T(8,128)}, f32[256,2048]{1,0:T(8,128)}, f32[512,128]{1,0:T(8,128)}) custom-call(f32[256,2048]{1,0:T(8,128)} %x_ref.4, f32[256,2048]{1,0:T(8,128)} %dy_ref.5, f32[256,32]{1,0:T(8,128)} %bitcast.88, f32[256,32]{1,0:T(8,128)} %bitcast.87, f32[8,4,256]{2,1,0:T(4,128)} %reshape.413.inner_ref, f32[8,4,256]{2,1,0:T(4,128)} %reshape.414.rates_ref, ...), custom_call_target="tpu_custom_call" | custom-call | flops 2415919104 | bytes 8388608 | tf_op jit(solution)/shard_map/local/pallas_call | solution.py:245
  52.2 3.5 %collective-permute-start.1 = (f32[32,128]{1,0:T(8,128)S(1)}, f32[32,128]{1,0:T(8,128)S(1)}, u32[]{:S(2)}, u32[]{:S(2)}) collective-permute-start(f32[32,128]{1,0:T(8,128)S(1)} %add.162), channel_id=1, source_target_pairs={{0,4},{2,6},{4,0},{6,2},{8,12},{10,14},{12,8},{14,10},{16,20},{18,... | collective-permute-start | bytes 49160 | tf_op jit(solution)/shard_map/ppermute | solution.py:128
  56.9 7.7 %collective-permute-start.2 = (f32[32,128]{1,0:T(8,128)S(1)}, f32[32,128]{1,0:T(8,128)S(1)}, u32[]{:S(2)}, u32[]{:S(2)}) collective-permute-start(f32[32,128]{1,0:T(8,128)S(1)} %add.163), channel_id=1, source_target_pairs={{0,8},{2,10},{4,12},{6,14},{8,0},{10,2},{12,4},{14,6},{16,24},{18,... | collective-permute-start | bytes 49160 | tf_op jit(solution)/shard_map/ppermute | solution.py:128
  65.7 15.2 %collective-permute-start.3 = (f32[32,128]{1,0:T(8,128)S(1)}, f32[32,128]{1,0:T(8,128)S(1)}, u32[]{:S(2)}, u32[]{:S(2)}) collective-permute-start(f32[32,128]{1,0:T(8,128)S(1)} %add.164), channel_id=1, source_target_pairs={{0,16},{2,18},{4,20},{6,22},{8,24},{10,26},{12,28},{14,30},{16,0},... | collective-permute-start | bytes 49160 | tf_op jit(solution)/shard_map/ppermute | solution.py:128
  81.0 1.4 broadcast_select_fusion.2
  82.7 2.5 collective-permute-start.6
  85.6 17.6 %collective-permute-start.4 = (f32[32,128]{1,0:T(8,128)S(1)}, f32[32,128]{1,0:T(8,128)S(1)}, u32[]{:S(2)}, u32[]{:S(2)}) collective-permute-start(f32[32,128]{1,0:T(8,128)S(1)} %add.165), channel_id=1, source_target_pairs={{0,32},{2,34},{4,36},{6,38},{8,40},{10,42},{12,44},{14,46},{16,48}... | collective-permute-start | bytes 49160 | tf_op jit(solution)/shard_map/ppermute | solution.py:128
  103.3 5.3 %collective-permute-done.6 = f32[2,32,2048]{2,1,0:T(8,128)S(1)} collective-permute-done((f32[2,32,2048]{2,1,0:T(8,128)S(1)}, f32[2,32,2048]{2,1,0:T(8,128)S(1)}, u32[]{:S(2)}, u32[]{:S(2)}) %collective-permute-start.6) | collective-permute-done | bytes 524320 | tf_op jit(solution)/shard_map/ppermute | solution.py:149
  108.8 7.7 %collective-permute-start.7 = (f32[2,16,2048]{2,1,0:T(8,128)S(1)}, f32[2,16,2048]{2,1,0:T(8,128)S(1)}, u32[]{:S(2)}, u32[]{:S(2)}) collective-permute-start(f32[2,16,2048]{2,1,0:T(8,128)S(1)} %broadcast_select_fusion.15), channel_id=1, source_target_pairs={{0,8},{2,10},{4,12},{6,14},{8,0},{10,2},{12,4},{14,6},{16,24},{18,... | collective-permute-start | bytes 786440 | tf_op jit(solution)/shard_map/ppermute | solution.py:149
  117.0 23.4 %collective-permute-done.7 = f32[2,16,2048]{2,1,0:T(8,128)S(1)} collective-permute-done((f32[2,16,2048]{2,1,0:T(8,128)S(1)}, f32[2,16,2048]{2,1,0:T(8,128)S(1)}, u32[]{:S(2)}, u32[]{:S(2)}) %collective-permute-start.7) | collective-permute-done | bytes 262176 | tf_op jit(solution)/shard_map/ppermute | solution.py:149
  140.5 22.2 %collective-permute-start.10 = (f32[16,2048]{1,0:T(8,128)S(1)}, f32[16,2048]{1,0:T(8,128)S(1)}, u32[]{:S(2)}, u32[]{:S(2)}) collective-permute-start(f32[16,2048]{1,0:T(8,128)S(1)} %get-tuple-element.32), channel_id=1, source_target_pairs={{0,48},{2,50},{4,52},{6,54},{8,56},{10,58},{12,60},{14,62},{16,0},... | collective-permute-start | bytes 393224 | tf_op jit(solution)/shard_map/ppermute | solution.py:165
  163.8 10.1 %collective-permute-start.8 = (f32[16,2048]{1,0:T(8,128)S(1)}, f32[16,2048]{1,0:T(8,128)S(1)}, u32[]{:S(2)}, u32[]{:S(2)}) collective-permute-start(f32[16,2048]{1,0:T(8,128)S(1)} %get-tuple-element.72), channel_id=1, source_target_pairs={{0,16},{2,18},{4,20},{6,22},{8,24},{10,26},{12,28},{14,30},{16,32}... | collective-permute-start | bytes 393224 | tf_op jit(solution)/shard_map/ppermute | solution.py:165
  174.0 7.5 %collective-permute-done.10 = f32[16,2048]{1,0:T(8,128)S(1)} collective-permute-done((f32[16,2048]{1,0:T(8,128)S(1)}, f32[16,2048]{1,0:T(8,128)S(1)}, u32[]{:S(2)}, u32[]{:S(2)}) %collective-permute-start.10) | collective-permute-done | bytes 131104 | tf_op jit(solution)/shard_map/ppermute | solution.py:165
  181.5 24.3 %collective-permute-done.9 = f32[16,2048]{1,0:T(8,128)S(1)} collective-permute-done((f32[16,2048]{1,0:T(8,128)S(1)}, f32[16,2048]{1,0:T(8,128)S(1)}, u32[]{:S(2)}, u32[]{:S(2)}) %collective-permute-start.9) | collective-permute-done | bytes 131104 | tf_op jit(solution)/shard_map/ppermute | solution.py:165
  206.1 14.4 %collective-permute-done.11 = f32[2,16,2048]{2,1,0:T(8,128)S(1)} collective-permute-done((f32[2,16,2048]{2,1,0:T(8,128)S(1)}, f32[2,16,2048]{2,1,0:T(8,128)S(1)}, u32[]{:S(2)}, u32[]{:S(2)}) %collective-permute-start.11) | collective-permute-done | bytes 262176 | tf_op jit(solution)/shard_map/ppermute | solution.py:183
  221.0 23.6 %collective-permute-done.12 = f32[2,32,2048]{2,1,0:T(8,128)S(1)} collective-permute-done((f32[2,32,2048]{2,1,0:T(8,128)S(1)}, f32[2,32,2048]{2,1,0:T(8,128)S(1)}, u32[]{:S(2)}, u32[]{:S(2)}) %collective-permute-start.12) | collective-permute-done | bytes 524320 | tf_op jit(solution)/shard_map/ppermute | solution.py:183
  245.6 24.2 %collective-permute-done.13 = f32[2,64,2048]{2,1,0:T(8,128)S(1)} collective-permute-done((f32[2,64,2048]{2,1,0:T(8,128)S(1)}, f32[2,64,2048]{2,1,0:T(8,128)S(1)}, u32[]{:S(2)}, u32[]{:S(2)}) %collective-permute-start.13) | collective-permute-done | bytes 1048608 | tf_op jit(solution)/shard_map/ppermute | solution.py:183
  270.2 10.7 %finish.1 = (f32[256,2048]{1,0:T(8,128)}, f32[256,2048]{1,0:T(8,128)}, f32[512,128]{1,0:T(8,128)S(1)}) custom-call(f32[256,2048]{1,0:T(8,128)S(1)} %copy-done, f32[256,2048]{1,0:T(8,128)S(1)} %copy-done.1, f32[256,32]{1,0:T(8,128)S(1)} %copy-done.5, f32[256,32]{1,0:T(8,128)S(1)} %copy-done.4, f32[256,128]{1,0:T(8,128)S(1)} %copy-done.6, ...), custom_call_target="tpu_custom_call" | custom-call | flops 1610612736 | bytes 14680064 | tf_op jit(solution)/shard_map/finish/pallas_call | solution.py:249
  280.8 1.3 collective-permute-start.14
  282.2 1.2 collective-permute-done.14
  (106 shorter events, 13.0 us)
Async XLA Ops:
  1.6 50.5 %collective-permute-start = (f32[32,128]{1,0:T(8,128)S(1)}, f32[32,128]{1,0:T(8,128)S(1)}, u32[]{:S(2)}, u32[]{:S(2)}) collective-permute-start(f32[32,128]{1,0:T(8,128)S(1)} %dynamic_update_slice.5), channel_id=1, source_target_pairs={{0,2},{2,0},{4,6},{6,4},{8,10},{10,8},{12,14},{14,12},{16,18},{18,... | collective-permute-start | bytes 49160 | tf_op jit(solution)/shard_map/ppermute | solution.py:128
  18.5 62.5 %collective-permute-start.5 = (f32[2,64,2048]{2,1,0:T(8,128)S(1)}, f32[2,64,2048]{2,1,0:T(8,128)}, u32[]{:S(2)}, u32[]{:S(2)}) collective-permute-start(f32[2,64,2048]{2,1,0:T(8,128)S(1)} %slice_select_fusion.1), channel_id=1, source_target_pairs={{0,2},{2,0},{4,6},{6,4},{8,10},{10,8},{12,14},{14,12},{16,18},{18,... | collective-permute-start | bytes 3145736 | tf_op jit(solution)/shard_map/ppermute | solution.py:149
  21.1 59.8 %copy-start.9 = (f32[2,128,2048]{2,1,0:T(8,128)S(1)}, f32[2,128,2048]{2,1,0:T(8,128)}, u32[]{:S(2)}) copy-start(f32[2,128,2048]{2,1,0:T(8,128)} %states.1) | copy-start | bytes 6291460
  52.2 4.7 %collective-permute-start.1 = (f32[32,128]{1,0:T(8,128)S(1)}, f32[32,128]{1,0:T(8,128)S(1)}, u32[]{:S(2)}, u32[]{:S(2)}) collective-permute-start(f32[32,128]{1,0:T(8,128)S(1)} %add.162), channel_id=1, source_target_pairs={{0,4},{2,6},{4,0},{6,2},{8,12},{10,14},{12,8},{14,10},{16,20},{18,... | collective-permute-start | bytes 49160 | tf_op jit(solution)/shard_map/ppermute | solution.py:128
  56.9 8.8 %collective-permute-start.2 = (f32[32,128]{1,0:T(8,128)S(1)}, f32[32,128]{1,0:T(8,128)S(1)}, u32[]{:S(2)}, u32[]{:S(2)}) collective-permute-start(f32[32,128]{1,0:T(8,128)S(1)} %add.163), channel_id=1, source_target_pairs={{0,8},{2,10},{4,12},{6,14},{8,0},{10,2},{12,4},{14,6},{16,24},{18,... | collective-permute-start | bytes 49160 | tf_op jit(solution)/shard_map/ppermute | solution.py:128
  65.7 19.9 %collective-permute-start.3 = (f32[32,128]{1,0:T(8,128)S(1)}, f32[32,128]{1,0:T(8,128)S(1)}, u32[]{:S(2)}, u32[]{:S(2)}) collective-permute-start(f32[32,128]{1,0:T(8,128)S(1)} %add.164), channel_id=1, source_target_pairs={{0,16},{2,18},{4,20},{6,22},{8,24},{10,26},{12,28},{14,30},{16,0},... | collective-permute-start | bytes 49160 | tf_op jit(solution)/shard_map/ppermute | solution.py:128
  82.7 25.8 %collective-permute-start.6 = (f32[2,32,2048]{2,1,0:T(8,128)S(1)}, f32[2,32,2048]{2,1,0:T(8,128)S(1)}, u32[]{:S(2)}, u32[]{:S(2)}) collective-permute-start(f32[2,32,2048]{2,1,0:T(8,128)S(1)} %broadcast_select_fusion.9), channel_id=1, source_target_pairs={{0,4},{2,6},{4,0},{6,2},{8,12},{10,14},{12,8},{14,10},{16,20},{18,... | collective-permute-start | bytes 1572872 | tf_op jit(solution)/shard_map/ppermute | solution.py:149
  85.6 30.8 %collective-permute-start.4 = (f32[32,128]{1,0:T(8,128)S(1)}, f32[32,128]{1,0:T(8,128)S(1)}, u32[]{:S(2)}, u32[]{:S(2)}) collective-permute-start(f32[32,128]{1,0:T(8,128)S(1)} %add.165), channel_id=1, source_target_pairs={{0,32},{2,34},{4,36},{6,38},{8,40},{10,42},{12,44},{14,46},{16,48}... | collective-permute-start | bytes 49160 | tf_op jit(solution)/shard_map/ppermute | solution.py:128
  108.8 31.7 %collective-permute-start.7 = (f32[2,16,2048]{2,1,0:T(8,128)S(1)}, f32[2,16,2048]{2,1,0:T(8,128)S(1)}, u32[]{:S(2)}, u32[]{:S(2)}) collective-permute-start(f32[2,16,2048]{2,1,0:T(8,128)S(1)} %broadcast_select_fusion.15), channel_id=1, source_target_pairs={{0,8},{2,10},{4,12},{6,14},{8,0},{10,2},{12,4},{14,6},{16,24},{18,... | collective-permute-start | bytes 786440 | tf_op jit(solution)/shard_map/ppermute | solution.py:149
  140.5 41.0 %collective-permute-start.10 = (f32[16,2048]{1,0:T(8,128)S(1)}, f32[16,2048]{1,0:T(8,128)S(1)}, u32[]{:S(2)}, u32[]{:S(2)}) collective-permute-start(f32[16,2048]{1,0:T(8,128)S(1)} %get-tuple-element.32), channel_id=1, source_target_pairs={{0,48},{2,50},{4,52},{6,54},{8,56},{10,58},{12,60},{14,62},{16,0},... | collective-permute-start | bytes 393224 | tf_op jit(solution)/shard_map/ppermute | solution.py:165
  162.8 43.0 %collective-permute-start.9 = (f32[16,2048]{1,0:T(8,128)S(1)}, f32[16,2048]{1,0:T(8,128)S(1)}, u32[]{:S(2)}, u32[]{:S(2)}) collective-permute-start(f32[16,2048]{1,0:T(8,128)S(1)} %get-tuple-element.71), channel_id=1, source_target_pairs={{0,32},{2,34},{4,36},{6,38},{8,40},{10,42},{12,44},{14,46},{16,48}... | collective-permute-start | bytes 393224 | tf_op jit(solution)/shard_map/ppermute | solution.py:165
  163.8 42.0 %collective-permute-start.8 = (f32[16,2048]{1,0:T(8,128)S(1)}, f32[16,2048]{1,0:T(8,128)S(1)}, u32[]{:S(2)}, u32[]{:S(2)}) collective-permute-start(f32[16,2048]{1,0:T(8,128)S(1)} %get-tuple-element.72), channel_id=1, source_target_pairs={{0,16},{2,18},{4,20},{6,22},{8,24},{10,26},{12,28},{14,30},{16,32}... | collective-permute-start | bytes 393224 | tf_op jit(solution)/shard_map/ppermute | solution.py:165
  205.9 14.6 %collective-permute-start.11 = (f32[2,16,2048]{2,1,0:T(8,128)S(1)}, f32[2,16,2048]{2,1,0:T(8,128)S(1)}, u32[]{:S(2)}, u32[]{:S(2)}) collective-permute-start(f32[2,16,2048]{2,1,0:T(8,128)S(1)} %fusion.23), channel_id=1, source_target_pairs={{0,8},{2,10},{4,12},{6,14},{8,0},{10,2},{12,4},{14,6},{16,24},{18,... | collective-permute-start | bytes 786440 | tf_op jit(solution)/shard_map/ppermute | solution.py:183
  220.9 23.7 %collective-permute-start.12 = (f32[2,32,2048]{2,1,0:T(8,128)S(1)}, f32[2,32,2048]{2,1,0:T(8,128)S(1)}, u32[]{:S(2)}, u32[]{:S(2)}) collective-permute-start(f32[2,32,2048]{2,1,0:T(8,128)S(1)} %fusion.16), channel_id=1, source_target_pairs={{0,4},{2,6},{4,0},{6,2},{8,12},{10,14},{12,8},{14,10},{16,20},{18,... | collective-permute-start | bytes 1572872 | tf_op jit(solution)/shard_map/ppermute | solution.py:183
  245.1 25.0 %copy-start.4 = (f32[256,32]{1,0:T(8,128)S(1)}, f32[256,32]{1,0:T(8,128)}, u32[]{:S(2)}) copy-start(f32[256,32]{1,0:T(8,128)} %get-tuple-element.73.growth_ref) | copy-start | bytes 98308
  245.1 25.0 %copy-start.5 = (f32[256,32]{1,0:T(8,128)S(1)}, f32[256,32]{1,0:T(8,128)}, u32[]{:S(2)}) copy-start(f32[256,32]{1,0:T(8,128)} %get-tuple-element.74.tail_ref) | copy-start | bytes 98308
  245.1 25.0 %copy-start.6 = (f32[256,128]{1,0:T(8,128)S(1)}, f32[256,128]{1,0:T(8,128)}, u32[]{:S(2)}) copy-start(f32[256,128]{1,0:T(8,128)} %b_ref.5) | copy-start | bytes 393220
  245.1 25.0 %copy-start.7 = (f32[256,128]{1,0:T(8,128)S(1)}, f32[256,128]{1,0:T(8,128)}, u32[]{:S(2)}) copy-start(f32[256,128]{1,0:T(8,128)} %c_ref.5) | copy-start | bytes 393220
  245.1 25.0 %copy-start.8 = (f32[512,128]{1,0:T(8,128)S(1)}, f32[512,128]{1,0:T(8,128)}, u32[]{:S(2)}) copy-start(f32[512,128]{1,0:T(8,128)} %get-tuple-element.24.terms_ref) | copy-start | bytes 786436
  245.2 24.9 %copy-start.2 = (f32[256,2048]{1,0:T(8,128)S(1)}, f32[256,2048]{1,0:T(8,128)}, u32[]{:S(2)}) copy-start(f32[256,2048]{1,0:T(8,128)} %get-tuple-element.22.y_ref) | copy-start | bytes 6291460
  245.2 24.9 %copy-start.3 = (f32[256,2048]{1,0:T(8,128)S(1)}, f32[256,2048]{1,0:T(8,128)}, u32[]{:S(2)}) copy-start(f32[256,2048]{1,0:T(8,128)} %get-tuple-element.23.gx_ref) | copy-start | bytes 6291460
  245.4 24.8 %copy-start = (f32[256,2048]{1,0:T(8,128)S(1)}, f32[256,2048]{1,0:T(8,128)}, u32[]{:S(2)}) copy-start(f32[256,2048]{1,0:T(8,128)} %x_ref.4) | copy-start | bytes 6291460
  245.4 24.4 %collective-permute-start.13 = (f32[2,64,2048]{2,1,0:T(8,128)S(1)}, f32[2,64,2048]{2,1,0:T(8,128)S(1)}, u32[]{:S(2)}, u32[]{:S(2)}) collective-permute-start(f32[2,64,2048]{2,1,0:T(8,128)S(1)} %fusion.6), channel_id=1, source_target_pairs={{0,2},{2,0},{4,6},{6,4},{8,10},{10,8},{12,14},{14,12},{16,18},{18,... | collective-permute-start | bytes 3145736 | tf_op jit(solution)/shard_map/ppermute | solution.py:183
  280.8 2.5 collective-permute-start.14
  (5 other events, 52.4 us)

commit v2 on v1

--- a/solution.py
+++ b/solution.py
@@ -26,20 +26,25 @@
 TN = (((0,), (0,)), ((), ()))
 
 
-def spread(columns, first, width, lanes):
-    heads = columns.shape[1]
-    row = lax.broadcasted_iota(jnp.int32, (heads, lanes), 0)
-    lane = lax.broadcasted_iota(jnp.int32, (heads, lanes), 1)
-    chosen = jnp.where(row == first + lane // width, 1.0, 0.0).astype(jnp.float32)
-    return jnp.dot(columns, chosen, precision=HIGHEST, preferred_element_type=jnp.float32)
-
-
-def states_kernel(width, x_ref, dy_ref, tail_ref, growth_ref, b_ref, c_ref, out_ref):
-    first = pl.program_id(0) * (LANES // width)
-    xs = x_ref[...] * spread(tail_ref[...], first, width, LANES)
-    ys = dy_ref[...] * spread(growth_ref[...], first, width, LANES)
-    out_ref[0] = dot3(halves(b_ref[...]), halves(xs), TN)
-    out_ref[1] = dot3(halves(c_ref[...]), halves(ys), TN)
+def spread(columns, width):
+    tokens, heads = columns.shape
+    lane = lax.broadcasted_iota(jnp.int32, (tokens, 2 * width), 1)
+    pairs = [jnp.where(lane < width, columns[:, i : i + 1], columns[:, i + 1 : i + 2]) for i in range(0, heads, 2)]
+    return jnp.concatenate(pairs, axis=1)
+
+
+def scales(inner_ref, rates_ref, width):
+    inner = inner_ref[0]
+    tail = jnp.exp(jnp.minimum(inner[-1:] - inner, 0.0)) * rates_ref[0]
+    return spread(tail, width), spread(jnp.exp(inner), width)
+
+
+def states_kernel(width, x_ref, dy_ref, inner_ref, rates_ref, b_ref, c_ref, out_ref):
+    tail, growth = scales(inner_ref, rates_ref, width)
+    for i, (keys_ref, rows) in enumerate(((b_ref, x_ref[...] * tail), (c_ref, dy_ref[...] * growth))):
+        state = dot3(halves(keys_ref[...]), halves(rows), TN)
+        for j in range(LANES // 128):
+            out_ref[i, :, j] = state[:, j * 128 : (j + 1) * 128].reshape(-1, 8, 128)
 
 
 def local_kernel(width, x_ref, dy_ref, inner_t_ref, rates_t_ref, inner_ref, rates_ref, skip_ref, b_ref, c_ref, y_ref, gx_ref, keys_ref, cb_ref, bc_ref, sum_ref):
@@ -70,8 +75,8 @@
             zero = jnp.zeros((), jnp.bfloat16)
             x_own = tuple(jnp.where(mine, part, zero) for part in x_parts)
             dy_own = tuple(jnp.where(mine, part, zero) for part in dy_parts)
-            down = spread(inner_t_ref[...], step * per + i, tokens, tokens)
-            dt_down = spread(rates_t_ref[...], step * per + i, tokens, tokens)
+            down = jnp.broadcast_to(inner_t_ref[0, :, i : i + 1], (tokens, tokens))
+            dt_down = jnp.broadcast_to(rates_t_ref[0, :, i : i + 1], (tokens, tokens))
             across = inner_ref[0, i : i + 1, :]
             gap = down - across
             within = jnp.where(row >= col, jnp.exp(jnp.minimum(gap, 0.0)), 0.0) * rates_ref[0, i : i + 1, :]
@@ -90,13 +95,19 @@
         keys_ref[tokens:] = dot3(parts, halves(b_ref[...]))
 
 
-def finish_kernel(width, x_ref, dy_ref, tail_ref, growth_ref, b_ref, c_ref, low_ref, high_ref, y_ref, gx_ref, terms_ref, out_ref, grad_ref, keys_ref):
+def finish_kernel(width, x_ref, dy_ref, inner_ref, rates_ref, b_ref, c_ref, low_ref, high_ref, y_ref, gx_ref, terms_ref, out_ref, grad_ref, keys_ref):
     step = pl.program_id(0)
     tokens = x_ref.shape[0]
-    first = step * (LANES // width)
-    tail = spread(tail_ref[...], first, width, LANES)
-    growth = spread(growth_ref[...], first, width, LANES)
-    entering, adjoint = (halves(jnp.concatenate([low_ref[i], high_ref[i]], axis=0)) for i in range(2))
+    tail, growth = scales(inner_ref, rates_ref, width)
+
+    def state(i):
+        rows = [
+            jnp.concatenate([ref[i, :, j].reshape(-1, 128) for j in range(LANES // 128)], axis=1)
+            for ref in (low_ref, high_ref)
+        ]
+        return halves(jnp.concatenate(rows, axis=0))
+
+    entering, adjoint = state(0), state(1)
     out_ref[...] = y_ref[...] + growth * dot3(halves(c_ref[...]), entering)
     grad_ref[...] = gx_ref[...] + tail * dot3(halves(b_ref[...]), adjoint)
 
@@ -112,65 +123,53 @@
     return pl.BlockSpec(shape, lambda i: (0,) * len(shape))
 
 
-def span(weights, table):
-    return jnp.exp(jnp.dot(weights, table, precision=HIGHEST))
-
-
-def exchange(states, log_decay, spread_lanes, axis, meanwhile):
+def exchange(states, log_decay, axis, meanwhile):
     size, mine = lax.axis_size(axis), lax.axis_index(axis)
-    heads = log_decay.shape[0]
-    table = jnp.zeros((size, 128), jnp.float32)
-    table = lax.dynamic_update_slice(table, jnp.pad(log_decay, (0, 128 - heads))[None], (mine, 0))
-    seg = jnp.arange(size)
-    steps = size.bit_length() - 1
-    tables = []
-    for k in range(steps):
-        table = table + lax.ppermute(table, axis, [(i, i ^ (1 << k)) for i in range(size)])
-        tables.append(table)
-
-    def weights(masks, known):
-        rows = span(jnp.stack(masks).astype(jnp.float32), known)
-        return jnp.dot(rows, spread_lanes, precision=HIGHEST)
+    tiles = log_decay.shape[0]
+
+    def send(values, logs, pairs):
+        got = lax.ppermute(jnp.concatenate([values.reshape(-1, 128), logs], axis=0), axis, pairs)
+        return got[:-tiles].reshape(values.shape), got[-tiles:]
+
+    def decay(logs):
+        return jnp.exp(logs)[None, :, None, :]
 
     kept, sides = [], []
-    now = states
+    now, logs = states, log_decay
     for k in range(LEVELS):
         pairs = [(i, i ^ (1 << k)) for i in range(size)]
         right = ((mine >> k) & 1) == 1
-        base = (mine >> (k + 1)) << (k + 1)
-        half = 1 << k
-        both = weights(
-            [(seg >= base) & (seg < base + half), (seg >= base + half) & (seg < base + 2 * half)], tables[k]
-        )
-        over_left, over_right = both[0:1], both[1:2]
         rows = now.shape[1] // 2
         low, high = now[:, :rows], now[:, rows:]
         own = jnp.where(right, high, low)
-        got = lax.ppermute(jnp.where(right, low, high), axis, pairs)
+        got, other = send(jnp.where(right, low, high), logs, pairs)
+        left_logs, right_logs = jnp.where(right, other, logs), jnp.where(right, logs, other)
+        over_left, over_right = decay(left_logs), decay(right_logs)
         left_part, right_part = jnp.where(right, got, own), jnp.where(right, own, got)
         now = jnp.stack(
             [over_right * left_part[0] + right_part[0], left_part[1] + over_left * right_part[1]]
         )
+        logs = left_logs + right_logs
         kept.append((left_part[0], right_part[1], over_left, over_right))
         sides.append((pairs, right))
 
     block = 1 << LEVELS
     count = size // block
     place = mine // block
+    received, sources = [], []
+    for d in range(1, count):
+        pairs = [(i, (i + block * d) % size) for i in range(size)]
+        received.append(send(jnp.where(place + d < count, now[0], now[1]), logs, pairs))
+        sources.append((place - d) % count)
+    aside = meanwhile()
     forward = jnp.zeros_like(now[0])
     backward = jnp.zeros_like(now[0])
-    masks, received = [], []
     for d in range(1, count):
-        pairs = [(i, (i + block * d) % size) for i in range(size)]
-        received.append(lax.ppermute(jnp.where(place + d < count, now[0], now[1]), axis, pairs))
-        source = (place - d) % count
-        first, last = jnp.minimum(source, place), jnp.maximum(source, place)
-        masks.append((seg // block > first) & (seg // block < last))
-    between = weights(masks, tables[-1])
-    aside = meanwhile(now)
-    received, aside = lax.optimization_barrier((received, aside))
-    for d in range(1, count):
-        term = between[d - 1 : d] * received[d - 1]
+        first, last = jnp.minimum(sources[d - 1], place), jnp.maximum(sources[d - 1], place)
+        between = jnp.zeros_like(logs)
+        for (_, other), source in zip(received, sources, strict=True):
+            between = between + jnp.where((source > first) & (source < last), other, 0.0)
+        term = decay(between) * received[d - 1][0]
         forward = forward + jnp.where(place >= d, term, 0.0)
         backward = backward + jnp.where(place >= d, 0.0, term)
 
@@ -199,18 +198,17 @@
     upto = jnp.triu(jnp.ones((tokens, tokens), jnp.float32))
     inner = jnp.dot(logs, upto, precision=HIGHEST)
     total = jnp.sum(logs, axis=1)
-    inner_t = inner.T
-    rates_t = rates.T
-    growth_t = jnp.exp(inner_t)
-    tail_t = jnp.exp(jnp.minimum(total[None, :] - inner_t, 0.0)) * rates_t
-    head_of = jnp.arange(lanes) // width
-    spread_lanes = (jnp.arange(128)[:, None] == head_of[None, :]).astype(jnp.float32)
-    skip_lanes = jnp.dot(jnp.pad(skip, (0, 128 - heads))[None], spread_lanes, precision=HIGHEST)
+    inner_rows, rates_rows = inner.reshape(grid, per, tokens), rates.reshape(grid, per, tokens)
+    inner_t, rates_t = jnp.swapaxes(inner_rows, 1, 2), jnp.swapaxes(rates_rows, 1, 2)
+
+    def on_lanes(of_heads):
+        lane = jnp.arange(lanes).reshape(lanes // 128, 128, 1)
+        return jnp.sum(jnp.where(lane // width == jnp.arange(heads), of_heads, 0.0), axis=2)
 
     tile = pl.BlockSpec((tokens, LANES), lambda i: (0, i))
-    state_tile = pl.BlockSpec((2, state_size, LANES), lambda i: (0, 0, i))
-    half_tile = pl.BlockSpec((2, state_size // 2, LANES), lambda i: (0, 0, i))
-    columns = whole((tokens, heads))
+    state_tile = pl.BlockSpec((2, state_size // 8, LANES // 128, 8, 128), lambda i: (0, 0, i, 0, 0))
+    half_tile = pl.BlockSpec((2, state_size // 16, LANES // 128, 8, 128), lambda i: (0, 0, i, 0, 0))
+    columns = pl.BlockSpec((1, tokens, per), lambda i: (i, 0, 0))
     keys = whole((tokens, state_size))
     big = jax.ShapeDtypeStruct((tokens, lanes), jnp.float32)
     params = pltpu.CompilerParams(dimension_semantics=("arbitrary",))
@@ -220,11 +218,11 @@
         grid=(grid,),
         in_specs=[tile, tile, columns, columns, keys, keys],
         out_specs=state_tile,
-        out_shape=jax.ShapeDtypeStruct((2, state_size, lanes), jnp.float32),
+        out_shape=jax.ShapeDtypeStruct((2, state_size // 8, lanes // 128, 8, 128), jnp.float32),
         compiler_params=params,
         cost_estimate=pl.CostEstimate(flops=12 * tokens * state_size * lanes, bytes_accessed=6 << 20, transcendentals=0),
         name="states",
-    )(inputs, grad_out, tail_t, growth_t, keys_b, keys_c)
+    )(inputs, grad_out, inner_t, rates_t, keys_b, keys_c)
 
     small = pl.BlockSpec((1, per, tokens), lambda i: (i, 0, 0))
     local = pl.pallas_call(
@@ -238,13 +236,12 @@
         cost_estimate=pl.CostEstimate(flops=18 * tokens * tokens * lanes, bytes_accessed=8 << 20, transcendentals=2 * tokens * tokens * heads),
         name="local",
     )
-    by_step = inner.reshape(grid, per, tokens), rates.reshape(grid, per, tokens)
-
-    def meanwhile(after):
-        x, _ = lax.optimization_barrier((inputs, after))
-        return local(x, grad_out, inner_t, rates_t, *by_step, skip_lanes, keys_b, keys_c)
-
-    (low, high), (y, gx, terms) = exchange(states, total, spread_lanes, "seq", meanwhile)
+    skip_lanes = on_lanes(skip).reshape(1, lanes)
+
+    def meanwhile():
+        return local(inputs, grad_out, inner_t, rates_t, inner_rows, rates_rows, skip_lanes, keys_b, keys_c)
+
+    (low, high), (y, gx, terms) = exchange(states, on_lanes(total), "seq", meanwhile)
 
     output, grad_x, key_terms = pl.pallas_call(
         functools.partial(finish_kernel, width),
@@ -255,7 +252,7 @@
         compiler_params=pltpu.CompilerParams(dimension_semantics=("arbitrary",), vmem_limit_bytes=20 << 20),
         cost_estimate=pl.CostEstimate(flops=24 * tokens * state_size * lanes, bytes_accessed=14 << 20, transcendentals=0),
         name="finish",
-    )(inputs, grad_out, tail_t, growth_t, keys_b, keys_c, low, high, y, gx, terms)
+    )(inputs, grad_out, inner_t, rates_t, keys_b, keys_c, low, high, y, gx, terms)
     cores = lax.axis_size("head")
     summed = key_terms
     for d in range(1, cores):

time: 285 us -> 272 us (0.954)
  starting transfers between devices: 92.3 us -> 65.1 us
  waiting for transfers between devices: 125 us -> 145 us
  Pallas kernels: 51.1 us -> 34.6 us
  local copies, waits for them, and re-layouts: 3.41 us -> 12 us
  other arithmetic: 6.7 us -> 11.9 us
  matrix products: 4.42 us -> 1.11 us
    ppermute x11 -> x6, waiting for transfers between devices: 61.6 us -> 93.3 us  [send(): lax.ppermute(jnp.concatenate([values.reshape(-1, 128), logs], axis=0), ax...]
    ppermute x11 -> x6, starting transfers between devices: 90.5 us -> 63.4 us  [send(): lax.ppermute(jnp.concatenate([values.reshape(-1, 128), logs], axis=0), ax...]
    pallas_call x1, Pallas kernels: 30.9 us -> 17.7 us  [meanwhile(): local(inputs, grad_out, inner_t, rates_t, inner_rows, rates_rows, skip_la...]
    ppermute x3, waiting for transfers between devices: 62.2 us -> 50.8 us  [exchange(): got = lax.ppermute(jnp.where(right, to_left, to_right), axis, pairs)]
    unnamed x29 -> x44, local copies, waits for them, and re-layouts: 0.93 us -> 5.15 us
    dot_general x9 -> x0, matrix products: 3.29 us -> none  [the longest x4 1.76 us: weights(): return jnp.dot(rows, spread_lanes, precision=HIGHEST)]
    pallas_call x1, Pallas kernels: 10.7 us -> 7.74 us  [body(): pl.pallas_call(functools.partial(finish_kernel, width), grid=(grid,), in_...]
  transfers between devices with their start and end apart: 15 -> 10, of which waited for: 10 -> 9; matrix products, arithmetic and copies ran while one was open for 4% -> 0% of each run, Pallas kernels for 14% -> 7%
where the time goes in v2:
time: 272 us; the launch traced here: 271 us
  waiting for transfers between devices  145 us (53%)
  starting transfers between devices  65.1 us (24%)
  Pallas kernels  34.6 us (13%)
  local copies, waits for them, and re-layouts  12 us (4%)
  other arithmetic  11.9 us (4%)
    ppermute x6, waiting for transfers between devices, send(): lax.ppermute(jnp.concatenate([values.reshape(-1, 128), logs], axis=0), ax...  93.3 us
    ppermute x6, starting transfers between devices, send(): lax.ppermute(jnp.concatenate([values.reshape(-1, 128), logs], axis=0), ax...  63.4 us
    ppermute x3, waiting for transfers between devices, exchange(): got = lax.ppermute(jnp.where(right, to_left, to_right), axis, pairs)  50.8 us
    pallas_call x1, Pallas kernels, meanwhile(): local(inputs, grad_out, inner_t, rates_t, inner_rows, rates_rows, skip_la...  17.7 us
    pallas_call x1, Pallas kernels, body(): pl.pallas_call(functools.partial(states_kernel, width), grid=(grid,), in_...  9.17 us
    pallas_call x1, Pallas kernels, body(): pl.pallas_call(functools.partial(finish_kernel, width), grid=(grid,), in_...  7.74 us
  transfers between devices with their start and end apart: 10, of which 9 were waited for; matrix products, arithmetic and copies ran while one was open for 0% of the time, Pallas kernels for 7%

profile of v2, /device:TPU:37, one launch (start us, length us, event | category | flops | bytes accessed | tf_op | source)
XLA Modules:
  0.0 271.0 jit_solution(6234787424027196861)
XLA Ops:
  3.6 1.4 copy.16
  4.9 1.4 copy.15
  6.3 9.2 %states.1 = f32[2,16,16,8,128]{4,3,2,1,0:T(8,128)} custom-call(f32[256,2048]{1,0:T(8,128)} %x_ref.5, f32[256,2048]{1,0:T(8,128)} %dy_ref.5, f32[8,256,4]{2,1,0:T(8,128)} %bitcast.61, f32[8,256,4]{2,1,0:T(8,128)} %bitcast.58, f32[256,128]{1,0:T(8,128)} %b_ref.5, f32[256,128]{1,0:T(8,128)} %c_ref.5), custom_call_target="tpu_custom_call" | custom-call | flops 805306368 | bytes 6291456 | tf_op jit(solution)/shard_map/states/pallas_call | solution.py:216
  15.5 1.7 slice_select_fusion.1
  18.0 2.8 %collective-permute-start = (f32[2064,128]{1,0:T(8,128)S(1)}, f32[2064,128]{1,0:T(8,128)}, u32[]{:S(2)}, u32[]{:S(2)}) collective-permute-start(f32[2064,128]{1,0:T(8,128)S(1)} %pad_maximum_fusion), channel_id=1, source_target_pairs={{0,2},{2,0},{4,6},{6,4},{8,10},{10,8},{12,14},{14,12},{16,18},{18,... | collective-permute-start | bytes 3170312 | tf_op jit(solution)/shard_map/ppermute | solution.py:131
  20.7 12.4 %collective-permute-done = f32[2064,128]{1,0:T(8,128)} collective-permute-done((f32[2064,128]{1,0:T(8,128)S(1)}, f32[2064,128]{1,0:T(8,128)}, u32[]{:S(2)}, u32[]{:S(2)}) %collective-permute-start) | collective-permute-done | bytes 1056800 | tf_op jit(solution)/shard_map/ppermute | solution.py:131
  36.5 14.2 %collective-permute-start.1 = (f32[1040,128]{1,0:T(8,128)}, f32[1040,128]{1,0:T(8,128)S(1)}, u32[]{:S(2)}, u32[]{:S(2)}) collective-permute-start(f32[1040,128]{1,0:T(8,128)} %pad_maximum_fusion.3), channel_id=1, source_target_pairs={{0,4},{2,6},{4,0},{6,2},{8,12},{10,14},{12,8},{14,10},{16,20},{18,... | collective-permute-start | bytes 1597448 | tf_op jit(solution)/shard_map/ppermute | solution.py:131
  50.7 21.1 %collective-permute-done.1 = f32[1040,128]{1,0:T(8,128)S(1)} collective-permute-done((f32[1040,128]{1,0:T(8,128)}, f32[1040,128]{1,0:T(8,128)S(1)}, u32[]{:S(2)}, u32[]{:S(2)}) %collective-permute-start.1) | collective-permute-done | bytes 532512 | tf_op jit(solution)/shard_map/ppermute | solution.py:131
  74.3 9.9 %collective-permute-start.2 = (f32[528,128]{1,0:T(8,128)}, f32[528,128]{1,0:T(8,128)S(1)}, u32[]{:S(2)}, u32[]{:S(2)}) collective-permute-start(f32[528,128]{1,0:T(8,128)} %pad_maximum_fusion.7), channel_id=1, source_target_pairs={{0,8},{2,10},{4,12},{6,14},{8,0},{10,2},{12,4},{14,6},{16,24},{18,... | collective-permute-start | bytes 811016 | tf_op jit(solution)/shard_map/ppermute | solution.py:131
  84.2 23.6 %collective-permute-done.2 = f32[528,128]{1,0:T(8,128)S(1)} collective-permute-done((f32[528,128]{1,0:T(8,128)}, f32[528,128]{1,0:T(8,128)S(1)}, u32[]{:S(2)}, u32[]{:S(2)}) %collective-permute-start.2) | collective-permute-done | bytes 270368 | tf_op jit(solution)/shard_map/ppermute | solution.py:131
  108.1 15.3 %collective-permute-start.3 = (f32[272,128]{1,0:T(8,128)S(1)}, f32[272,128]{1,0:T(8,128)S(1)}, u32[]{:S(2)}, u32[]{:S(2)}) collective-permute-start(f32[272,128]{1,0:T(8,128)S(1)} %get-tuple-element.79), channel_id=1, source_target_pairs={{0,16},{2,18},{4,20},{6,22},{8,24},{10,26},{12,28},{14,30},{16,32}... | collective-permute-start | bytes 417800 | tf_op jit(solution)/shard_map/ppermute | solution.py:131
  123.4 16.6 %collective-permute-start.4 = (f32[272,128]{1,0:T(8,128)S(1)}, f32[272,128]{1,0:T(8,128)S(1)}, u32[]{:S(2)}, u32[]{:S(2)}) collective-permute-start(f32[272,128]{1,0:T(8,128)S(1)} %get-tuple-element.80), channel_id=1, source_target_pairs={{0,32},{2,34},{4,36},{6,38},{8,40},{10,42},{12,44},{14,46},{16,48}... | collective-permute-start | bytes 417800 | tf_op jit(solution)/shard_map/ppermute | solution.py:131
  139.9 4.6 %collective-permute-start.5 = (f32[272,128]{1,0:T(8,128)S(1)}, f32[272,128]{1,0:T(8,128)}, u32[]{:S(2)}, u32[]{:S(2)}) collective-permute-start(f32[272,128]{1,0:T(8,128)S(1)} %get-tuple-element.81), channel_id=1, source_target_pairs={{0,48},{2,50},{4,52},{6,54},{8,56},{10,58},{12,60},{14,62},{16,0},... | collective-permute-start | bytes 417800 | tf_op jit(solution)/shard_map/ppermute | solution.py:131
  144.6 5.8 %collective-permute-done.3 = f32[272,128]{1,0:T(8,128)S(1)} collective-permute-done((f32[272,128]{1,0:T(8,128)S(1)}, f32[272,128]{1,0:T(8,128)S(1)}, u32[]{:S(2)}, u32[]{:S(2)}) %collective-permute-start.3) | collective-permute-done | bytes 139296 | tf_op jit(solution)/shard_map/ppermute | solution.py:131
  150.4 30.4 %collective-permute-done.4 = f32[272,128]{1,0:T(8,128)S(1)} collective-permute-done((f32[272,128]{1,0:T(8,128)S(1)}, f32[272,128]{1,0:T(8,128)S(1)}, u32[]{:S(2)}, u32[]{:S(2)}) %collective-permute-start.4) | collective-permute-done | bytes 139296 | tf_op jit(solution)/shard_map/ppermute | solution.py:131
  182.8 22.3 %collective-permute-done.6 = f32[2,2,16,8,128]{4,3,2,1,0:T(8,128)S(1)} collective-permute-done((f32[2,2,16,8,128]{4,3,2,1,0:T(8,128)S(1)}, f32[2,2,16,8,128]{4,3,2,1,0:T(8,128)S(1)}, u32[]{:S(2)}, u32[]{:S(2)}) %collective-permute-start.6) | collective-permute-done | bytes 262176 | tf_op jit(solution)/shard_map/ppermute | solution.py:182
  205.5 21.9 %collective-permute-done.7 = f32[2,4,16,8,128]{4,3,2,1,0:T(8,128)S(1)} collective-permute-done((f32[2,4,16,8,128]{4,3,2,1,0:T(8,128)S(1)}, f32[2,4,16,8,128]{4,3,2,1,0:T(8,128)S(1)}, u32[]{:S(2)}, u32[]{:S(2)}) %collective-permute-start.7) | collective-permute-done | bytes 524320 | tf_op jit(solution)/shard_map/ppermute | solution.py:182
  229.1 1.4 fusion.1
  230.6 17.7 %local.1 = (f32[256,2048]{1,0:T(8,128)}, f32[256,2048]{1,0:T(8,128)}, f32[512,128]{1,0:T(8,128)}) custom-call(f32[256,2048]{1,0:T(8,128)} %x_ref.5, f32[256,2048]{1,0:T(8,128)} %dy_ref.5, f32[8,256,4]{2,1,0:T(8,128)} %bitcast.62, f32[8,256,4]{2,1,0:T(8,128)} %bitcast.59, f32[8,4,256]{2,1,0:T(4,128)} %copy-done.20, f32[8,4,256]{2,1,0:T(4,128)} %copy-done.19, ...), custom_call_target="tpu_custom_call" | custom-call | flops 2415919104 | bytes 8388608 | tf_op jit(solution)/shard_map/local/pallas_call | solution.py:242
  248.4 6.6 %collective-permute-done.8 = f32[2,8,16,8,128]{4,3,2,1,0:T(8,128)} collective-permute-done((f32[2,8,16,8,128]{4,3,2,1,0:T(8,128)}, f32[2,8,16,8,128]{4,3,2,1,0:T(8,128)}, u32[]{:S(2)}, u32[]{:S(2)}) %collective-permute-start.8) | collective-permute-done | bytes 1048608 | tf_op jit(solution)/shard_map/ppermute | solution.py:182
  255.0 1.8 broadcast_select_fusion
  256.8 1.6 copy-done.4
  258.4 1.6 copy-done.5
  260.0 7.7 %finish.1 = (f32[256,2048]{1,0:T(8,128)}, f32[256,2048]{1,0:T(8,128)}, f32[512,128]{1,0:T(8,128)S(1)}) custom-call(f32[256,2048]{1,0:T(8,128)S(1)} %copy-done.2, f32[256,2048]{1,0:T(8,128)S(1)} %copy-done.3, f32[8,256,4]{2,1,0:T(8,128)S(1)} %bitcast.63, f32[8,256,4]{2,1,0:T(8,128)S(1)} %bitcast.60, f32[256,128]{1,0:T(8,128)S(1)} %copy-done.6, ...), custom_call_target="tpu_custom_call" | custom-call | flops 1610612736 | bytes 14680064 | tf_op jit(solution)/shard_map/finish/pallas_call | solution.py:246
  (98 shorter events, 17.1 us)
Async XLA Ops:
  1.4 14.0 %copy-start.19 = (f32[8,4,256]{2,1,0:T(4,128)}, f32[8,4,256]{2,1,0:T(4,128)S(1)}, u32[]{:S(2)}) copy-start(f32[8,4,256]{2,1,0:T(4,128)S(1)} %reshape.333.rates_ref) | copy-start | bytes 98308
  3.5 11.9 %copy-start.20 = (f32[8,4,256]{2,1,0:T(4,128)}, f32[8,4,256]{2,1,0:T(4,128)S(1)}, u32[]{:S(2)}) copy-start(f32[8,4,256]{2,1,0:T(4,128)S(1)} %reshape.332.inner_ref) | copy-start | bytes 98308
  15.5 1.7 copy-start.21
  17.9 16.5 %copy-start.9 = (f32[2,16,16,8,128]{4,3,2,1,0:T(8,128)S(1)}, f32[2,16,16,8,128]{4,3,2,1,0:T(8,128)}, u32[]{:S(2)}) copy-start(f32[2,16,16,8,128]{4,3,2,1,0:T(8,128)} %states.1) | copy-start | bytes 6291460
  18.0 15.2 %collective-permute-start = (f32[2064,128]{1,0:T(8,128)S(1)}, f32[2064,128]{1,0:T(8,128)}, u32[]{:S(2)}, u32[]{:S(2)}) collective-permute-start(f32[2064,128]{1,0:T(8,128)S(1)} %pad_maximum_fusion), channel_id=1, source_target_pairs={{0,2},{2,0},{4,6},{6,4},{8,10},{10,8},{12,14},{14,12},{16,18},{18,... | collective-permute-start | bytes 3170312 | tf_op jit(solution)/shard_map/ppermute | solution.py:131
  36.5 35.3 %collective-permute-start.1 = (f32[1040,128]{1,0:T(8,128)}, f32[1040,128]{1,0:T(8,128)S(1)}, u32[]{:S(2)}, u32[]{:S(2)}) collective-permute-start(f32[1040,128]{1,0:T(8,128)} %pad_maximum_fusion.3), channel_id=1, source_target_pairs={{0,4},{2,6},{4,0},{6,2},{8,12},{10,14},{12,8},{14,10},{16,20},{18,... | collective-permute-start | bytes 1597448 | tf_op jit(solution)/shard_map/ppermute | solution.py:131
  74.3 33.6 %collective-permute-start.2 = (f32[528,128]{1,0:T(8,128)}, f32[528,128]{1,0:T(8,128)S(1)}, u32[]{:S(2)}, u32[]{:S(2)}) collective-permute-start(f32[528,128]{1,0:T(8,128)} %pad_maximum_fusion.7), channel_id=1, source_target_pairs={{0,8},{2,10},{4,12},{6,14},{8,0},{10,2},{12,4},{14,6},{16,24},{18,... | collective-permute-start | bytes 811016 | tf_op jit(solution)/shard_map/ppermute | solution.py:131
  108.1 42.3 %collective-permute-start.3 = (f32[272,128]{1,0:T(8,128)S(1)}, f32[272,128]{1,0:T(8,128)S(1)}, u32[]{:S(2)}, u32[]{:S(2)}) collective-permute-start(f32[272,128]{1,0:T(8,128)S(1)} %get-tuple-element.79), channel_id=1, source_target_pairs={{0,16},{2,18},{4,20},{6,22},{8,24},{10,26},{12,28},{14,30},{16,32}... | collective-permute-start | bytes 417800 | tf_op jit(solution)/shard_map/ppermute | solution.py:131
  123.4 57.4 %collective-permute-start.4 = (f32[272,128]{1,0:T(8,128)S(1)}, f32[272,128]{1,0:T(8,128)S(1)}, u32[]{:S(2)}, u32[]{:S(2)}) collective-permute-start(f32[272,128]{1,0:T(8,128)S(1)} %get-tuple-element.80), channel_id=1, source_target_pairs={{0,32},{2,34},{4,36},{6,38},{8,40},{10,42},{12,44},{14,46},{16,48}... | collective-permute-start | bytes 417800 | tf_op jit(solution)/shard_map/ppermute | solution.py:131
  139.9 40.9 %collective-permute-start.5 = (f32[272,128]{1,0:T(8,128)S(1)}, f32[272,128]{1,0:T(8,128)}, u32[]{:S(2)}, u32[]{:S(2)}) collective-permute-start(f32[272,128]{1,0:T(8,128)S(1)} %get-tuple-element.81), channel_id=1, source_target_pairs={{0,48},{2,50},{4,52},{6,54},{8,56},{10,58},{12,60},{14,62},{16,0},... | collective-permute-start | bytes 417800 | tf_op jit(solution)/shard_map/ppermute | solution.py:131
  182.6 22.4 %collective-permute-start.6 = (f32[2,2,16,8,128]{4,3,2,1,0:T(8,128)S(1)}, f32[2,2,16,8,128]{4,3,2,1,0:T(8,128)S(1)}, u32[]{:S(2)}, u32[]{:S(2)}) collective-permute-start(f32[2,2,16,8,128]{4,3,2,1,0:T(8,128)S(1)} %fusion.13), channel_id=1, source_target_pairs={{0,8},{2,10},{4,12},{6,14},{8,0},{10,2},{12,4},{14,6},{16,24},{18,... | collective-permute-start | bytes 786440 | tf_op jit(solution)/shard_map/ppermute | solution.py:182
  205.4 22.0 %collective-permute-start.7 = (f32[2,4,16,8,128]{4,3,2,1,0:T(8,128)S(1)}, f32[2,4,16,8,128]{4,3,2,1,0:T(8,128)S(1)}, u32[]{:S(2)}, u32[]{:S(2)}) collective-permute-start(f32[2,4,16,8,128]{4,3,2,1,0:T(8,128)S(1)} %fusion.6), channel_id=1, source_target_pairs={{0,4},{2,6},{4,0},{6,2},{8,12},{10,14},{12,8},{14,10},{16,20},{18,... | collective-permute-start | bytes 1572872 | tf_op jit(solution)/shard_map/ppermute | solution.py:182
  230.4 24.5 %collective-permute-start.8 = (f32[2,8,16,8,128]{4,3,2,1,0:T(8,128)}, f32[2,8,16,8,128]{4,3,2,1,0:T(8,128)}, u32[]{:S(2)}, u32[]{:S(2)}) collective-permute-start(f32[2,8,16,8,128]{4,3,2,1,0:T(8,128)} %fusion.1), channel_id=1, source_target_pairs={{0,2},{2,0},{4,6},{6,4},{8,10},{10,8},{12,14},{14,12},{16,18},{18,... | collective-permute-start | bytes 3145736 | tf_op jit(solution)/shard_map/ppermute | solution.py:182
  230.6 24.4 %copy-start.13 = (f32[1,8,16,8,128]{4,3,2,1,0:T(8,128)S(1)}, f32[1,8,16,8,128]{4,3,2,1,0:T(8,128)}, u32[]{:S(2)}) copy-start(f32[1,8,16,8,128]{4,3,2,1,0:T(8,128)} %copy-done.12) | copy-start | bytes 1572868
  230.6 24.4 %copy-start.15 = (f32[1,8,16,8,128]{4,3,2,1,0:T(8,128)S(1)}, f32[1,8,16,8,128]{4,3,2,1,0:T(8,128)}, u32[]{:S(2)}) copy-start(f32[1,8,16,8,128]{4,3,2,1,0:T(8,128)} %copy-done.14) | copy-start | bytes 1572868
  230.6 26.2 %copy-start.3 = (f32[256,2048]{1,0:T(8,128)S(1)}, f32[256,2048]{1,0:T(8,128)}, u32[]{:S(2)}) copy-start(f32[256,2048]{1,0:T(8,128)} %dy_ref.5) | copy-start | bytes 6291460
  248.3 8.5 %copy-start = (f32[8,4,256]{1,2,0:T(8,128)S(1)}, f32[8,4,256]{1,2,0:T(8,128)}, u32[]{:S(2)}) copy-start(f32[8,4,256]{1,2,0:T(8,128)} %copy.16) | copy-start | bytes 98308
  248.3 8.5 %copy-start.1 = (f32[8,4,256]{1,2,0:T(8,128)S(1)}, f32[8,4,256]{1,2,0:T(8,128)}, u32[]{:S(2)}) copy-start(f32[8,4,256]{1,2,0:T(8,128)} %copy.15) | copy-start | bytes 98308
  248.3 8.5 %copy-start.2 = (f32[256,2048]{1,0:T(8,128)S(1)}, f32[256,2048]{1,0:T(8,128)}, u32[]{:S(2)}) copy-start(f32[256,2048]{1,0:T(8,128)} %x_ref.5) | copy-start | bytes 6291460
  248.3 8.5 %copy-start.6 = (f32[256,128]{1,0:T(8,128)S(1)}, f32[256,128]{1,0:T(8,128)}, u32[]{:S(2)}) copy-start(f32[256,128]{1,0:T(8,128)} %b_ref.5) | copy-start | bytes 393220
  248.4 8.5 %copy-start.7 = (f32[256,128]{1,0:T(8,128)S(1)}, f32[256,128]{1,0:T(8,128)}, u32[]{:S(2)}) copy-start(f32[256,128]{1,0:T(8,128)} %c_ref.5) | copy-start | bytes 393220
  248.4 8.5 %copy-start.8 = (f32[512,128]{1,0:T(8,128)S(1)}, f32[512,128]{1,0:T(8,128)}, u32[]{:S(2)}) copy-start(f32[512,128]{1,0:T(8,128)} %get-tuple-element.12.terms_ref) | copy-start | bytes 786436
  256.8 1.6 copy-start.4
  267.8 2.5 collective-permute-start.9
  (8 other events, 10.5 us)

commit v3 on v2

--- a/solution.py
+++ b/solution.py
@@ -157,19 +157,20 @@
     count = size // block
     place = mine // block
     received, sources = [], []
-    for d in range(1, count):
+    offsets = sorted(range(1, count), key=lambda d: -min(d, count - d))
+    for d in offsets:
         pairs = [(i, (i + block * d) % size) for i in range(size)]
         received.append(send(jnp.where(place + d < count, now[0], now[1]), logs, pairs))
         sources.append((place - d) % count)
     aside = meanwhile()
     forward = jnp.zeros_like(now[0])
     backward = jnp.zeros_like(now[0])
-    for d in range(1, count):
-        first, last = jnp.minimum(sources[d - 1], place), jnp.maximum(sources[d - 1], place)
+    for d, (values, _), origin in zip(offsets, received, sources, strict=True):
+        first, last = jnp.minimum(origin, place), jnp.maximum(origin, place)
         between = jnp.zeros_like(logs)
         for (_, other), source in zip(received, sources, strict=True):
             between = between + jnp.where((source > first) & (source < last), other, 0.0)
-        term = decay(between) * received[d - 1][0]
+        term = decay(between) * values
         forward = forward + jnp.where(place >= d, term, 0.0)
         backward = backward + jnp.where(place >= d, 0.0, term)
 

time: 272 us -> 272 us (level)
  waiting for transfers between devices: 145 us -> 142 us
  starting transfers between devices: 65.1 us -> 68 us
    ppermute x6, waiting for transfers between devices: 93.3 us -> 87.1 us  [send(): lax.ppermute(jnp.concatenate([values.reshape(-1, 128), logs], axis=0), ax...]
    ppermute x6, starting transfers between devices: 63.4 us -> 66.4 us  [send(): lax.ppermute(jnp.concatenate([values.reshape(-1, 128), logs], axis=0), ax...]
    ppermute x3, waiting for transfers between devices: 50.8 us -> 53.6 us  [exchange(): got = lax.ppermute(jnp.where(right, to_left, to_right), axis, pairs)]
  transfers between devices with their start and end apart: 10 -> 10, of which waited for: 9 -> 8; matrix products, arithmetic and copies ran while one was open for 0% -> 0% of each run, Pallas kernels for 7% -> 7%
where the time goes in v3:
time: 272 us; the launch traced here: 271 us
  waiting for transfers between devices  142 us (52%)
  starting transfers between devices  68 us (25%)
  Pallas kernels  34.6 us (13%)
  local copies, waits for them, and re-layouts  12 us (4%)
  other arithmetic  11.9 us (4%)
    ppermute x6, waiting for transfers between devices, send(): lax.ppermute(jnp.concatenate([values.reshape(-1, 128), logs], axis=0), ax...  87.1 us
    ppermute x6, starting transfers between devices, send(): lax.ppermute(jnp.concatenate([values.reshape(-1, 128), logs], axis=0), ax...  66.4 us
    ppermute x3, waiting for transfers between devices, exchange(): got = lax.ppermute(jnp.where(right, to_left, to_right), axis, pairs)  53.6 us
    pallas_call x1, Pallas kernels, meanwhile(): local(inputs, grad_out, inner_t, rates_t, inner_rows, rates_rows, skip_la...  17.7 us
    pallas_call x1, Pallas kernels, body(): pl.pallas_call(functools.partial(states_kernel, width), grid=(grid,), in_...  9.17 us
    pallas_call x1, Pallas kernels, body(): pl.pallas_call(functools.partial(finish_kernel, width), grid=(grid,), in_...  7.75 us
  transfers between devices with their start and end apart: 10, of which 8 were waited for; matrix products, arithmetic and copies ran while one was open for 0% of the time, Pallas kernels for 7%

profile of v3, /device:TPU:37, one launch (start us, length us, event | category | flops | bytes accessed | tf_op | source)
XLA Modules:
  0.0 270.7 jit_solution(12325613693391390259)
XLA Ops:
  3.6 1.4 copy.16
  4.9 1.4 copy.15
  6.3 9.2 %states.1 = f32[2,16,16,8,128]{4,3,2,1,0:T(8,128)} custom-call(f32[256,2048]{1,0:T(8,128)} %x_ref.5, f32[256,2048]{1,0:T(8,128)} %dy_ref.5, f32[8,256,4]{2,1,0:T(8,128)} %bitcast.61, f32[8,256,4]{2,1,0:T(8,128)} %bitcast.58, f32[256,128]{1,0:T(8,128)} %b_ref.5, f32[256,128]{1,0:T(8,128)} %c_ref.5), custom_call_target="tpu_custom_call" | custom-call | flops 805306368 | bytes 6291456 | tf_op jit(solution)/shard_map/states/pallas_call | solution.py:217
  15.5 1.7 slice_select_fusion.1
  18.0 2.8 %collective-permute-start = (f32[2064,128]{1,0:T(8,128)S(1)}, f32[2064,128]{1,0:T(8,128)}, u32[]{:S(2)}, u32[]{:S(2)}) collective-permute-start(f32[2064,128]{1,0:T(8,128)S(1)} %pad_maximum_fusion), channel_id=1, source_target_pairs={{0,2},{2,0},{4,6},{6,4},{8,10},{10,8},{12,14},{14,12},{16,18},{18,... | collective-permute-start | bytes 3170312 | tf_op jit(solution)/shard_map/ppermute | solution.py:131
  20.7 12.4 %collective-permute-done = f32[2064,128]{1,0:T(8,128)} collective-permute-done((f32[2064,128]{1,0:T(8,128)S(1)}, f32[2064,128]{1,0:T(8,128)}, u32[]{:S(2)}, u32[]{:S(2)}) %collective-permute-start) | collective-permute-done | bytes 1056800 | tf_op jit(solution)/shard_map/ppermute | solution.py:131
  36.5 14.2 %collective-permute-start.1 = (f32[1040,128]{1,0:T(8,128)}, f32[1040,128]{1,0:T(8,128)S(1)}, u32[]{:S(2)}, u32[]{:S(2)}) collective-permute-start(f32[1040,128]{1,0:T(8,128)} %pad_maximum_fusion.3), channel_id=1, source_target_pairs={{0,4},{2,6},{4,0},{6,2},{8,12},{10,14},{12,8},{14,10},{16,20},{18,... | collective-permute-start | bytes 1597448 | tf_op jit(solution)/shard_map/ppermute | solution.py:131
  50.7 21.1 %collective-permute-done.1 = f32[1040,128]{1,0:T(8,128)S(1)} collective-permute-done((f32[1040,128]{1,0:T(8,128)}, f32[1040,128]{1,0:T(8,128)S(1)}, u32[]{:S(2)}, u32[]{:S(2)}) %collective-permute-start.1) | collective-permute-done | bytes 532512 | tf_op jit(solution)/shard_map/ppermute | solution.py:131
  74.3 9.9 %collective-permute-start.2 = (f32[528,128]{1,0:T(8,128)}, f32[528,128]{1,0:T(8,128)S(1)}, u32[]{:S(2)}, u32[]{:S(2)}) collective-permute-start(f32[528,128]{1,0:T(8,128)} %pad_maximum_fusion.7), channel_id=1, source_target_pairs={{0,8},{2,10},{4,12},{6,14},{8,0},{10,2},{12,4},{14,6},{16,24},{18,... | collective-permute-start | bytes 811016 | tf_op jit(solution)/shard_map/ppermute | solution.py:131
  84.2 23.6 %collective-permute-done.2 = f32[528,128]{1,0:T(8,128)S(1)} collective-permute-done((f32[528,128]{1,0:T(8,128)}, f32[528,128]{1,0:T(8,128)S(1)}, u32[]{:S(2)}, u32[]{:S(2)}) %collective-permute-start.2) | collective-permute-done | bytes 270368 | tf_op jit(solution)/shard_map/ppermute | solution.py:131
  108.1 29.3 %collective-permute-start.3 = (f32[272,128]{1,0:T(8,128)S(1)}, f32[272,128]{1,0:T(8,128)S(1)}, u32[]{:S(2)}, u32[]{:S(2)}) collective-permute-start(f32[272,128]{1,0:T(8,128)S(1)} %get-tuple-element.79), channel_id=1, source_target_pairs={{0,32},{2,34},{4,36},{6,38},{8,40},{10,42},{12,44},{14,46},{16,48}... | collective-permute-start | bytes 417800 | tf_op jit(solution)/shard_map/ppermute | solution.py:131
  137.4 2.6 collective-permute-start.4
  140.0 7.6 %collective-permute-start.5 = (f32[272,128]{1,0:T(8,128)S(1)}, f32[272,128]{1,0:T(8,128)}, u32[]{:S(2)}, u32[]{:S(2)}) collective-permute-start(f32[272,128]{1,0:T(8,128)S(1)} %get-tuple-element.81), channel_id=1, source_target_pairs={{0,48},{2,50},{4,52},{6,54},{8,56},{10,58},{12,60},{14,62},{16,0},... | collective-permute-start | bytes 417800 | tf_op jit(solution)/shard_map/ppermute | solution.py:131
  147.6 30.0 %collective-permute-done.3 = f32[272,128]{1,0:T(8,128)S(1)} collective-permute-done((f32[272,128]{1,0:T(8,128)S(1)}, f32[272,128]{1,0:T(8,128)S(1)}, u32[]{:S(2)}, u32[]{:S(2)}) %collective-permute-start.3) | collective-permute-done | bytes 139296 | tf_op jit(solution)/shard_map/ppermute | solution.py:131
  179.6 25.1 %collective-permute-done.6 = f32[2,2,16,8,128]{4,3,2,1,0:T(8,128)S(1)} collective-permute-done((f32[2,2,16,8,128]{4,3,2,1,0:T(8,128)S(1)}, f32[2,2,16,8,128]{4,3,2,1,0:T(8,128)S(1)}, u32[]{:S(2)}, u32[]{:S(2)}) %collective-permute-start.6) | collective-permute-done | bytes 262176 | tf_op jit(solution)/shard_map/ppermute | solution.py:183
  205.1 22.0 %collective-permute-done.7 = f32[2,4,16,8,128]{4,3,2,1,0:T(8,128)S(1)} collective-permute-done((f32[2,4,16,8,128]{4,3,2,1,0:T(8,128)S(1)}, f32[2,4,16,8,128]{4,3,2,1,0:T(8,128)S(1)}, u32[]{:S(2)}, u32[]{:S(2)}) %collective-permute-start.7) | collective-permute-done | bytes 524320 | tf_op jit(solution)/shard_map/ppermute | solution.py:183
  228.7 1.4 fusion.1
  230.3 17.7 %local.1 = (f32[256,2048]{1,0:T(8,128)}, f32[256,2048]{1,0:T(8,128)}, f32[512,128]{1,0:T(8,128)}) custom-call(f32[256,2048]{1,0:T(8,128)} %x_ref.5, f32[256,2048]{1,0:T(8,128)} %dy_ref.5, f32[8,256,4]{2,1,0:T(8,128)} %bitcast.62, f32[8,256,4]{2,1,0:T(8,128)} %bitcast.59, f32[8,4,256]{2,1,0:T(4,128)} %copy-done.20, f32[8,4,256]{2,1,0:T(4,128)} %copy-done.19, ...), custom_call_target="tpu_custom_call" | custom-call | flops 2415919104 | bytes 8388608 | tf_op jit(solution)/shard_map/local/pallas_call | solution.py:243
  248.1 6.6 %collective-permute-done.8 = f32[2,8,16,8,128]{4,3,2,1,0:T(8,128)} collective-permute-done((f32[2,8,16,8,128]{4,3,2,1,0:T(8,128)}, f32[2,8,16,8,128]{4,3,2,1,0:T(8,128)}, u32[]{:S(2)}, u32[]{:S(2)}) %collective-permute-start.8) | collective-permute-done | bytes 1048608 | tf_op jit(solution)/shard_map/ppermute | solution.py:183
  254.7 1.8 broadcast_select_fusion
  256.5 1.6 copy-done.4
  258.1 1.6 copy-done.5
  259.7 7.8 %finish.1 = (f32[256,2048]{1,0:T(8,128)}, f32[256,2048]{1,0:T(8,128)}, f32[512,128]{1,0:T(8,128)S(1)}) custom-call(f32[256,2048]{1,0:T(8,128)S(1)} %copy-done.2, f32[256,2048]{1,0:T(8,128)S(1)} %copy-done.3, f32[8,256,4]{2,1,0:T(8,128)S(1)} %bitcast.63, f32[8,256,4]{2,1,0:T(8,128)S(1)} %bitcast.60, f32[256,128]{1,0:T(8,128)S(1)} %copy-done.6, ...), custom_call_target="tpu_custom_call" | custom-call | flops 1610612736 | bytes 14680064 | tf_op jit(solution)/shard_map/finish/pallas_call | solution.py:247
  267.5 1.3 collective-permute-start.9
  (98 shorter events, 15.7 us)
Async XLA Ops:
  1.4 14.0 %copy-start.19 = (f32[8,4,256]{2,1,0:T(4,128)}, f32[8,4,256]{2,1,0:T(4,128)S(1)}, u32[]{:S(2)}) copy-start(f32[8,4,256]{2,1,0:T(4,128)S(1)} %reshape.333.rates_ref) | copy-start | bytes 98308
  3.5 11.9 %copy-start.20 = (f32[8,4,256]{2,1,0:T(4,128)}, f32[8,4,256]{2,1,0:T(4,128)S(1)}, u32[]{:S(2)}) copy-start(f32[8,4,256]{2,1,0:T(4,128)S(1)} %reshape.332.inner_ref) | copy-start | bytes 98308
  15.5 1.7 copy-start.21
  17.9 16.5 %copy-start.9 = (f32[2,16,16,8,128]{4,3,2,1,0:T(8,128)S(1)}, f32[2,16,16,8,128]{4,3,2,1,0:T(8,128)}, u32[]{:S(2)}) copy-start(f32[2,16,16,8,128]{4,3,2,1,0:T(8,128)} %states.1) | copy-start | bytes 6291460
  18.0 15.2 %collective-permute-start = (f32[2064,128]{1,0:T(8,128)S(1)}, f32[2064,128]{1,0:T(8,128)}, u32[]{:S(2)}, u32[]{:S(2)}) collective-permute-start(f32[2064,128]{1,0:T(8,128)S(1)} %pad_maximum_fusion), channel_id=1, source_target_pairs={{0,2},{2,0},{4,6},{6,4},{8,10},{10,8},{12,14},{14,12},{16,18},{18,... | collective-permute-start | bytes 3170312 | tf_op jit(solution)/shard_map/ppermute | solution.py:131
  36.5 35.3 %collective-permute-start.1 = (f32[1040,128]{1,0:T(8,128)}, f32[1040,128]{1,0:T(8,128)S(1)}, u32[]{:S(2)}, u32[]{:S(2)}) collective-permute-start(f32[1040,128]{1,0:T(8,128)} %pad_maximum_fusion.3), channel_id=1, source_target_pairs={{0,4},{2,6},{4,0},{6,2},{8,12},{10,14},{12,8},{14,10},{16,20},{18,... | collective-permute-start | bytes 1597448 | tf_op jit(solution)/shard_map/ppermute | solution.py:131
  74.3 33.6 %collective-permute-start.2 = (f32[528,128]{1,0:T(8,128)}, f32[528,128]{1,0:T(8,128)S(1)}, u32[]{:S(2)}, u32[]{:S(2)}) collective-permute-start(f32[528,128]{1,0:T(8,128)} %pad_maximum_fusion.7), channel_id=1, source_target_pairs={{0,8},{2,10},{4,12},{6,14},{8,0},{10,2},{12,4},{14,6},{16,24},{18,... | collective-permute-start | bytes 811016 | tf_op jit(solution)/shard_map/ppermute | solution.py:131
  108.1 69.5 %collective-permute-start.3 = (f32[272,128]{1,0:T(8,128)S(1)}, f32[272,128]{1,0:T(8,128)S(1)}, u32[]{:S(2)}, u32[]{:S(2)}) collective-permute-start(f32[272,128]{1,0:T(8,128)S(1)} %get-tuple-element.79), channel_id=1, source_target_pairs={{0,32},{2,34},{4,36},{6,38},{8,40},{10,42},{12,44},{14,46},{16,48}... | collective-permute-start | bytes 417800 | tf_op jit(solution)/shard_map/ppermute | solution.py:131
  137.4 40.2 %collective-permute-start.4 = (f32[272,128]{1,0:T(8,128)S(1)}, f32[272,128]{1,0:T(8,128)S(1)}, u32[]{:S(2)}, u32[]{:S(2)}) collective-permute-start(f32[272,128]{1,0:T(8,128)S(1)} %get-tuple-element.80), channel_id=1, source_target_pairs={{0,16},{2,18},{4,20},{6,22},{8,24},{10,26},{12,28},{14,30},{16,32}... | collective-permute-start | bytes 417800 | tf_op jit(solution)/shard_map/ppermute | solution.py:131
  140.0 37.7 %collective-permute-start.5 = (f32[272,128]{1,0:T(8,128)S(1)}, f32[272,128]{1,0:T(8,128)}, u32[]{:S(2)}, u32[]{:S(2)}) collective-permute-start(f32[272,128]{1,0:T(8,128)S(1)} %get-tuple-element.81), channel_id=1, source_target_pairs={{0,48},{2,50},{4,52},{6,54},{8,56},{10,58},{12,60},{14,62},{16,0},... | collective-permute-start | bytes 417800 | tf_op jit(solution)/shard_map/ppermute | solution.py:131
  179.4 25.2 %collective-permute-start.6 = (f32[2,2,16,8,128]{4,3,2,1,0:T(8,128)S(1)}, f32[2,2,16,8,128]{4,3,2,1,0:T(8,128)S(1)}, u32[]{:S(2)}, u32[]{:S(2)}) collective-permute-start(f32[2,2,16,8,128]{4,3,2,1,0:T(8,128)S(1)} %fusion.13), channel_id=1, source_target_pairs={{0,8},{2,10},{4,12},{6,14},{8,0},{10,2},{12,4},{14,6},{16,24},{18,... | collective-permute-start | bytes 786440 | tf_op jit(solution)/shard_map/ppermute | solution.py:183
  205.0 22.1 %collective-permute-start.7 = (f32[2,4,16,8,128]{4,3,2,1,0:T(8,128)S(1)}, f32[2,4,16,8,128]{4,3,2,1,0:T(8,128)S(1)}, u32[]{:S(2)}, u32[]{:S(2)}) collective-permute-start(f32[2,4,16,8,128]{4,3,2,1,0:T(8,128)S(1)} %fusion.6), channel_id=1, source_target_pairs={{0,4},{2,6},{4,0},{6,2},{8,12},{10,14},{12,8},{14,10},{16,20},{18,... | collective-permute-start | bytes 1572872 | tf_op jit(solution)/shard_map/ppermute | solution.py:183
  230.1 24.5 %collective-permute-start.8 = (f32[2,8,16,8,128]{4,3,2,1,0:T(8,128)}, f32[2,8,16,8,128]{4,3,2,1,0:T(8,128)}, u32[]{:S(2)}, u32[]{:S(2)}) collective-permute-start(f32[2,8,16,8,128]{4,3,2,1,0:T(8,128)} %fusion.1), channel_id=1, source_target_pairs={{0,2},{2,0},{4,6},{6,4},{8,10},{10,8},{12,14},{14,12},{16,18},{18,... | collective-permute-start | bytes 3145736 | tf_op jit(solution)/shard_map/ppermute | solution.py:183
  230.3 24.4 %copy-start.13 = (f32[1,8,16,8,128]{4,3,2,1,0:T(8,128)S(1)}, f32[1,8,16,8,128]{4,3,2,1,0:T(8,128)}, u32[]{:S(2)}) copy-start(f32[1,8,16,8,128]{4,3,2,1,0:T(8,128)} %copy-done.12) | copy-start | bytes 1572868
  230.3 24.4 %copy-start.15 = (f32[1,8,16,8,128]{4,3,2,1,0:T(8,128)S(1)}, f32[1,8,16,8,128]{4,3,2,1,0:T(8,128)}, u32[]{:S(2)}) copy-start(f32[1,8,16,8,128]{4,3,2,1,0:T(8,128)} %copy-done.14) | copy-start | bytes 1572868
  230.3 26.2 %copy-start.3 = (f32[256,2048]{1,0:T(8,128)S(1)}, f32[256,2048]{1,0:T(8,128)}, u32[]{:S(2)}) copy-start(f32[256,2048]{1,0:T(8,128)} %dy_ref.5) | copy-start | bytes 6291460
  248.0 8.5 %copy-start = (f32[8,4,256]{1,2,0:T(8,128)S(1)}, f32[8,4,256]{1,2,0:T(8,128)}, u32[]{:S(2)}) copy-start(f32[8,4,256]{1,2,0:T(8,128)} %copy.16) | copy-start | bytes 98308
  248.0 8.5 %copy-start.1 = (f32[8,4,256]{1,2,0:T(8,128)S(1)}, f32[8,4,256]{1,2,0:T(8,128)}, u32[]{:S(2)}) copy-start(f32[8,4,256]{1,2,0:T(8,128)} %copy.15) | copy-start | bytes 98308
  248.0 8.5 %copy-start.2 = (f32[256,2048]{1,0:T(8,128)S(1)}, f32[256,2048]{1,0:T(8,128)}, u32[]{:S(2)}) copy-start(f32[256,2048]{1,0:T(8,128)} %x_ref.5) | copy-start | bytes 6291460
  248.0 8.5 %copy-start.6 = (f32[256,128]{1,0:T(8,128)S(1)}, f32[256,128]{1,0:T(8,128)}, u32[]{:S(2)}) copy-start(f32[256,128]{1,0:T(8,128)} %b_ref.5) | copy-start | bytes 393220
  248.0 8.5 %copy-start.7 = (f32[256,128]{1,0:T(8,128)S(1)}, f32[256,128]{1,0:T(8,128)}, u32[]{:S(2)}) copy-start(f32[256,128]{1,0:T(8,128)} %c_ref.5) | copy-start | bytes 393220
  248.1 8.5 %copy-start.8 = (f32[512,128]{1,0:T(8,128)S(1)}, f32[512,128]{1,0:T(8,128)}, u32[]{:S(2)}) copy-start(f32[512,128]{1,0:T(8,128)} %get-tuple-element.12.terms_ref) | copy-start | bytes 786436
  256.5 1.6 copy-start.4
  267.5 2.5 collective-permute-start.9
  (8 other events, 10.5 us)
